TPU v7x, 128 devices: a whole 4x4x4 slice. The times are simulated.
128 devices in a mesh: row: 8 (over y, x_hi), col: 16 (over x_lo, z, core).
Axes of the slice: x: 4 (x_hi: 2, x_lo: 2; x = x_hi * 2 + x_lo), y: 4, z: 4, core: 2. Of those that a mesh axis runs over, the one named last changes fastest.
Arguments:
- initial_field: float32 [1, 1024, 8192], P(None, 'row', 'col'), may hold values from -12 to 12
- information: float32 [1024, 8192], P('row', 'col'), may hold values from -24 to 24
- kappa_squared: float32 [1024, 8192], P('row', 'col'), may hold values from 0.05 to 2
- lumped_mass: float32 [1024, 8192], P('row', 'col'), may hold values from 0.5 to 2
- noise_seeds: int32 [8, 16, 2, 4, 1], P('row', 'col'), may hold values from 0 to 1073741823
- colour_order: int32 [4], replicated, may hold values from 0 to 3, each once
Outputs:
- final_field: float32 [1, 1024, 8192], P(None, 'row', 'col')
- energies: float32 [2, 4, 1], replicated
Inputs may be any that keep to these rules, and one draw needn't show every extreme that they name: `noise_seeds`: one seed for each tile of 128 x 512 nodes, sweep, colour phase and chain. `colour_order`: names each of the 4 block colours once.
All inputs are finite; a program needn't handle non-finite values.
Results may differ from a plain program's by a relative error of at most 0.0003.
Values sent between devices are 32-bit elements; how exact they have to be, the bound alone decides.
A program may use at most 128 MiB of HBM per device.

v0:
```python
import jax
import jax.numpy as jnp
from jax import lax
from jax.sharding import Mesh
from jax.sharding import PartitionSpec as P

SWEEPS = 2
COLOURS = 4
ROW = ("row_0", "row_1")
COL = ("col_0", "col_1", "col_2")
ROW_COL = ("row_0", "row_1", "col_0", "col_1", "col_2")


full_turn = 6.283185307179586
unit_step = 1.0 / 8388608.0
mix_factor = 73244475


def extended_2(shard, sides, width):
    edges = {}
    for axis, dim in sides:
        size, length = (lax.axis_size(axis), shard.shape[dim])
        up = [(i, (i + 1) % size) for i in range(size)]
        last = lax.slice_in_dim(shard, length - width, length, axis=dim)
        leading = lax.slice_in_dim(shard, 0, width, axis=dim)
        edges[dim] = (
            lax.ppermute(last, axis, up),
            lax.ppermute(leading, axis, [(b, a) for a, b in up]),
        )
    done = []
    for _, dim in sides:
        low, high = edges[dim]
        around = [(width, width) if d in done else (0, 0) for d in range(shard.ndim)]
        shard = jnp.concatenate([jnp.pad(low, around), shard, jnp.pad(high, around)], axis=dim)
        done.append(dim)
    return shard


def with_halo(block, sides, width):
    for axis, dim in sides:
        count = lax.axis_size(axis)
        forward = [(i, i + 1) for i in range(count - 1)]
        forward.append((count - 1, 0))
        backward = [(target, source) for source, target in forward]
        low = lax.ppermute(
            lax.slice_in_dim(block, block.shape[dim] - width, None, axis=dim), axis, forward
        )
        high = lax.ppermute(lax.slice_in_dim(block, 0, width, axis=dim), axis, backward)
        block = jnp.concatenate([low, block, high], axis=dim)
    return block


def one_axis_at_a_time(shard, axes):
    for axis in axes:
        shard = lax.psum(shard, axis)
    return shard


def crop_edges(source, amount):
    return source[..., amount : source.shape[-2] - amount, amount : source.shape[-1] - amount]


def stencil_sum(source):
    return (
        source[..., :-2, 1:-1]
        + source[..., 2:, 1:-1]
        + source[..., 1:-1, :-2]
        + source[..., 1:-1, 2:]
    )


def apply_precision(sample_field, stiffness, inverse):
    first_pass = stiffness * crop_edges(sample_field, 1) - stencil_sum(sample_field)
    scaled = inverse * first_pass
    return crop_edges(stiffness, 1) * crop_edges(scaled, 1) - stencil_sum(scaled)


def corners(source):
    return [
        source[..., first_index::2, second_index::2]
        for first_index in (0, 1)
        for second_index in (0, 1)
    ]


def join_corners(pieces):
    total = None
    for corner in range(4):
        piece = pieces[corner]
        row_parity, col_parity = (corner // 2, corner % 2)
        config = [(0, 0, 0)] * (piece.ndim - 2) + [
            (row_parity, 1 - row_parity, 1),
            (col_parity, 1 - col_parity, 1),
        ]
        padded = lax.pad(piece, jnp.zeros((), piece.dtype), config)
        total = padded if total is None else total + padded
    return total


def block_matrix(stiff_corners, inverse_corners, diagonal_corners):
    scaled = [stiff_corners[corner] * inverse_corners[corner] for corner in range(4)]
    matrix = [[None] * 4 for corner in range(4)]
    for corner in range(4):
        matrix[corner][corner] = diagonal_corners[corner]
    for first_index, second_index in ((0, 1), (0, 2), (1, 3), (2, 3)):
        element = -(scaled[first_index] + scaled[second_index])
        matrix[first_index][second_index] = element
        matrix[second_index][first_index] = element
    matrix[0][3] = inverse_corners[1] + inverse_corners[2]
    matrix[3][0] = matrix[0][3]
    matrix[1][2] = inverse_corners[0] + inverse_corners[3]
    matrix[2][1] = matrix[1][2]
    return matrix


def cholesky_rows(matrix):
    factor = [[None] * 4 for corner in range(4)]
    for first_index in range(4):
        for second_index in range(first_index + 1):
            running = matrix[first_index][second_index]
            for middle in range(second_index):
                running = running - factor[first_index][middle] * factor[second_index][middle]
            if first_index == second_index:
                factor[first_index][first_index] = jnp.sqrt(running)
            else:
                factor[first_index][second_index] = running / factor[second_index][second_index]
    return factor


def crop_matrix(matrix, amount):
    return [
        [None if element is None else crop_edges(element, amount) for element in matrix_row]
        for matrix_row in matrix
    ]


def resample(field_corners, applied_corners, info_corners, matrix, factor, noise_list):
    right_side = []
    for first_index in range(4):
        coupled = matrix[first_index][0] * field_corners[0]
        for second_index in range(1, 4):
            coupled = coupled + matrix[first_index][second_index] * field_corners[second_index]
        right_side.append(info_corners[first_index] - applied_corners[first_index] + coupled)
    forward = []
    for first_index in range(4):
        running = right_side[first_index]
        for second_index in range(first_index):
            running = running - factor[first_index][second_index] * forward[second_index]
        forward.append(running / factor[first_index][first_index])
    shifted = [forward[corner] + noise_list[corner] for corner in range(4)]
    result = [None] * 4
    for first_index in reversed(range(4)):
        running = shifted[first_index]
        for second_index in range(first_index + 1, 4):
            running = running - factor[second_index][first_index] * result[second_index]
        result[first_index] = running / factor[first_index][first_index]
    return result


def scramble(hashed):
    sixteen = jnp.full_like(hashed, 16)
    hashed = hashed ^ lax.shift_right_logical(hashed, sixteen)
    hashed = hashed * mix_factor
    hashed = hashed ^ lax.shift_right_logical(hashed, sixteen)
    hashed = hashed * mix_factor
    return hashed ^ lax.shift_right_logical(hashed, sixteen)


def gaussian(seed_nodes, offsets):
    first_hash = scramble(seed_nodes + 2 * offsets)
    second_hash = scramble(seed_nodes + 2 * offsets + 1)
    shift_nine = jnp.full_like(first_hash, 9)
    uniform_one = (
        lax.shift_right_logical(first_hash, shift_nine).astype(jnp.float32) + 1.0
    ) * unit_step
    uniform_two = lax.shift_right_logical(second_hash, shift_nine).astype(jnp.float32) * unit_step
    return jnp.sqrt(-2.0 * jnp.log(uniform_one)) * jnp.cos(full_turn * uniform_two)


def node_seeds(seed_table, which_rows, which_cols):
    result = jnp.zeros((seed_table.shape[-1], which_rows.shape[0], which_cols.shape[0]), jnp.int32)
    hit = (which_rows == 0)[:, None] & (which_cols == 0)[None, :]
    result = result + jnp.where(hit[None], seed_table[0, 0][:, None, None], 0)
    return result


def local(initial_field, information, kappa_squared, lumped_mass, noise_seeds, colour_order):
    chains, tile_rows, tile_cols = initial_field.shape
    total_rows = tile_rows * lax.axis_size(ROW)
    total_cols = tile_cols * lax.axis_size(COL)
    row_start = lax.axis_index(ROW) * tile_rows
    col_start = lax.axis_index(COL) * tile_cols
    kappa_ext, mass_ext = (
        extended_2(kappa_squared, ((ROW, 0), (COL, 1)), 1),
        extended_2(lumped_mass, ((ROW, 0), (COL, 1)), 1),
    )
    margin = 2
    info_margin = (information.shape[0] - tile_rows) // 2
    stiff_ext = kappa_ext * mass_ext + 4.0
    inverse_ext = 1.0 / mass_ext
    block_margin = margin - 2
    stiff_blocks = crop_edges(stiff_ext, 1)
    inverse_blocks = crop_edges(inverse_ext, 1)
    diagonal = stiff_blocks * stiff_blocks * inverse_blocks + stencil_sum(inverse_ext)
    matrix = block_matrix(corners(stiff_blocks), corners(inverse_blocks), corners(diagonal))
    factor = cholesky_rows(matrix)
    shrink_table = 1 - noise_seeds.shape[0] // 2

    def phase_tables(near_margin):
        half_rows = jnp.arange((tile_rows + 2 * near_margin) // 2, dtype=jnp.int32)
        half_cols = jnp.arange((tile_cols + 2 * near_margin) // 2, dtype=jnp.int32)
        block_rows = (row_start - near_margin) // 2 + half_rows
        block_cols = (col_start - near_margin) // 2 + half_cols
        block_colour = 2 * (block_rows % 2)[:, None] + (block_cols % 2)[None, :]
        offsets = []
        row_tiles = []
        col_tiles = []
        for corner in range(4):
            local_rows = 2 * half_rows + corner // 2 - near_margin
            local_cols = 2 * half_cols + corner % 2 - near_margin
            global_rows = (row_start + local_rows) % total_rows
            global_cols = (col_start + local_cols) % total_cols
            offsets.append(
                (global_rows % tile_rows)[:, None] * tile_cols + (global_cols % tile_cols)[None, :]
            )
            row_tiles.append(
                (local_rows >= 0).astype(jnp.int32)
                + (local_rows >= tile_rows).astype(jnp.int32)
                - shrink_table
            )
            col_tiles.append(
                (local_cols >= 0).astype(jnp.int32)
                + (local_cols >= tile_cols).astype(jnp.int32)
                - shrink_table
            )
        return (block_colour, offsets, row_tiles, col_tiles)

    def one_sweep(sweep_index, loop_state):
        sample_field, energies = loop_state
        seed_layer = lax.dynamic_index_in_dim(noise_seeds, sweep_index, 2, keepdims=False)
        for phase_index in range(COLOURS):
            extended = with_halo(sample_field, ((ROW, 1), (COL, 2)), 2)
            margin_now = (extended.shape[1] - tile_rows) // 2
            near_margin = margin_now - 2
            applied = apply_precision(
                extended,
                crop_edges(stiff_ext, margin - margin_now),
                crop_edges(inverse_ext, margin - margin_now),
            )
            inner_field = crop_edges(extended, margin_now)
            inner_applied = crop_edges(applied, near_margin)
            local_energy = jnp.sum(
                0.5 * inner_field * inner_applied - information * inner_field, axis=(1, 2)
            )
            energies = energies.at[sweep_index, phase_index].set(local_energy)
            dropped = (block_margin - near_margin) // 2
            block_colour, offsets, row_tiles, col_tiles = phase_tables(near_margin)
            chosen = block_colour == colour_order[phase_index]
            near_field = crop_edges(extended, 2)
            near_info = crop_edges(information, info_margin - near_margin)
            seed_table = seed_layer[:, :, phase_index, :]
            noise_list = []
            for corner in range(4):
                seeds_here = node_seeds(seed_table, row_tiles[corner], col_tiles[corner])
                noise_list.append(gaussian(seeds_here, offsets[corner]))
            before = corners(near_field)
            updated = resample(
                before,
                corners(applied),
                corners(near_info),
                crop_matrix(matrix, dropped),
                crop_matrix(factor, dropped),
                noise_list,
            )
            extended = join_corners(
                [jnp.where(chosen, updated[corner], before[corner]) for corner in range(4)]
            )
            sample_field = extended
        return (sample_field, energies)

    initial = (initial_field, jnp.zeros((SWEEPS, COLOURS, chains), jnp.float32))
    final_field, energies = lax.fori_loop(0, SWEEPS, one_sweep, initial)
    energies = one_axis_at_a_time(energies, ROW_COL) / (total_rows * total_cols)
    return (final_field, energies)


def solution(mesh):
    torus = Mesh(mesh.devices.reshape(4, 2, 2, 4, 2), ("row_0", "row_1", "col_0", "col_1", "col_2"))
    placed = (
        P(None, ROW, COL),
        P(ROW, COL),
        P(ROW, COL),
        P(ROW, COL),
        P(ROW, COL, None, None, None),
        P(),
    )
    return jax.shard_map(
        local, mesh=torus, in_specs=placed, out_specs=(P(None, ROW, COL), P()), check_vma=False
    )
```

profile of v0, /device:TPU:1, one launch (start us, length us, event | category | flops | bytes accessed | tf_op | source)
XLA Modules:
  0.0 585.1 jit_solution(5307698250823822969)
XLA Ops:
  1.7 3.1 collective-permute-start.16
  10.6 4.7 collective-permute-start.22
  15.3 3.7 collective-permute-done.19
  20.7 5.4 collective-permute-start.23
  56.4 494.9 %while.22 = (s32[]{:T(128)}, f32[1,128,512]{2,1,0:T(8,128)S(1)}, f32[2,4,1]{1,2,0:T(1,128)}, s32[]{:T(128)}, s32[]{:T(128)}, /*index=5*/s32[4]{0:T(128)S(1)}, f3...) while((s32[]{:T(128)}, f32[1,128,512]{2,1,0:T(8,128)S(1)}, ...), condition=%wide.region_9.10_spmd, body=%wide.region_0.9_spmd.sunk | while | flops 21103232 | bytes 64269184 | solution.py:282
  109.2 3.6 pad.717
  112.8 3.7 pad.718
  124.3 4.7 collective-permute-start.6
  131.3 2.9 slice.1687
  148.9 3.2 slice.1693
  153.3 3.2 fusion.565
  158.9 3.1 pad.719
  162.0 3.6 pad.720
  165.6 3.7 pad.721
  169.3 3.6 pad.722
  174.2 3.0 collective-permute-start.9
  181.0 3.8 collective-permute-start.10
  196.2 2.9 slice.1698
  204.7 3.2 slice.1701
  209.3 3.3 fusion.570
  214.9 4.5 pad.723
  219.4 3.7 pad.724
  223.0 3.6 pad.725
  226.7 3.6 pad.726
  231.7 3.0 collective-permute-start.13
  238.6 3.9 collective-permute-start.14
  260.7 3.2 slice.1706
  263.9 3.2 slice.1707
  267.1 3.2 slice.1708
  270.3 3.2 slice.1709
  292.3 3.6 pad.730
  303.1 3.0 collective-permute-start.1
  309.3 4.0 collective-permute-start.2
  356.3 3.6 pad.717
  360.0 3.7 pad.718
  371.2 4.9 collective-permute-start.6
  378.6 2.9 slice.1687
  396.1 3.2 slice.1693
  400.6 3.2 fusion.565
  406.2 3.1 pad.719
  409.3 3.6 pad.720
  412.9 3.7 pad.721
  416.5 3.6 pad.722
  421.5 3.0 collective-permute-start.9
  428.3 3.8 collective-permute-start.10
  443.4 2.9 slice.1698
  452.0 3.2 slice.1701
  456.6 3.3 fusion.570
  462.2 4.5 pad.723
  466.7 3.7 pad.724
  470.3 3.6 pad.725
  473.9 3.6 pad.726
  479.0 3.0 collective-permute-start.13
  485.8 3.9 collective-permute-start.14
  507.9 3.2 slice.1706
  511.2 3.2 slice.1707
  514.4 3.2 slice.1708
  517.6 3.2 slice.1709
  539.5 3.6 pad.730
  552.0 6.8 %psum.35 = f32[2,4,1]{1,2,0:T(1,128)S(1)} all-reduce(f32[2,4,1]{1,2,0:T(1,128)S(1)} %copy-done.55), channel_id=1, replica_groups=mesh['row_0'=4,'row_1'=2,'col_0'=2,'col_1'=4,'col_2'=2] {'row_0'}, use_global_device_ids=true, to_apply=%region_10.11 | all-reduce | flops 8 | bytes 64 | tf_op jit(solution)/shard_map/psum | solution.py:55
  558.8 5.3 psum.36
  564.1 4.0 psum.37
  568.1 11.0 %psum.38 = f32[2,4,1]{1,2,0:T(1,128)S(1)} all-reduce(f32[2,4,1]{1,2,0:T(1,128)S(1)} %psum.37), channel_id=1, replica_groups=mesh['row_0'=4,'row_1'=2,'col_0'=2,'col_1'=4,'col_2'=2] {'col_1'}, use_global_device_ids=true, to_apply=%region_13.14 | all-reduce | flops 8 | bytes 64 | tf_op jit(solution)/shard_map/psum | solution.py:55
  579.1 5.2 psum.39
  (470 shorter events, 344.3 us)
Async XLA Ops:
  1.7 13.6 %collective-permute-start.16 = (f32[128,1]{1,0:T(8,128)S(1)}, f32[128,1]{1,0:T(8,128)S(1)}, u32[]{:S(2)}, u32[]{:S(2)}) collective-permute-start(f32[128,1]{1,0:T(8,128)S(1)} %get-tuple-element.1180), channel_id=1, source_target_pairs={{0,1},{1,2},{2,3},{3,4},{4,5},{5,6},{6,7},{7,8},{8,9},{9,10},{10,1... | collective-permute-start | bytes 1544 | tf_op jit(solution)/shard_map/ppermute | solution.py:27
  4.7 22.3 %collective-permute-start.17 = (f32[1,512]{1,0:T(1,128)S(1)}, f32[1,512]{1,0:T(1,128)S(1)}, u32[]{:S(2)}, u32[]{:S(2)}) collective-permute-start(f32[1,512]{1,0:T(1,128)S(1)} %get-tuple-element.1178), channel_id=1, source_target_pairs={{0,16},{16,32},{32,48},{48,64},{64,80},{80,96},{96,112},{112,0},{1... | collective-permute-start | bytes 6152 | tf_op jit(solution)/shard_map/ppermute | solution.py:27
  7.5 19.5 %collective-permute-start.18 = (f32[1,512]{1,0:T(1,128)S(1)}, f32[1,512]{1,0:T(1,128)S(1)}, u32[]{:S(2)}, u32[]{:S(2)}) collective-permute-start(f32[1,512]{1,0:T(1,128)S(1)} %get-tuple-element.1179), channel_id=1, source_target_pairs={{16,0},{32,16},{48,32},{64,48},{80,64},{96,80},{112,96},{0,112},{1... | collective-permute-start | bytes 6152 | tf_op jit(solution)/shard_map/ppermute | solution.py:28
  10.0 17.0 %collective-permute-start.21 = (f32[1,512]{1,0:T(1,128)S(1)}, f32[1,512]{1,0:T(1,128)S(1)}, u32[]{:S(2)}, u32[]{:S(2)}) collective-permute-start(f32[1,512]{1,0:T(1,128)S(1)} %get-tuple-element.1176), channel_id=1, source_target_pairs={{0,16},{16,32},{32,48},{48,64},{64,80},{80,96},{96,112},{112,0},{1... | collective-permute-start | bytes 6152 | tf_op jit(solution)/shard_map/ppermute | solution.py:27
  10.6 16.4 %collective-permute-start.22 = (f32[1,512]{1,0:T(1,128)S(1)}, f32[1,512]{1,0:T(1,128)S(1)}, u32[]{:S(2)}, u32[]{:S(2)}) collective-permute-start(f32[1,512]{1,0:T(1,128)S(1)} %get-tuple-element.1177), channel_id=1, source_target_pairs={{16,0},{32,16},{48,32},{64,48},{80,64},{96,80},{112,96},{0,112},{1... | collective-permute-start | bytes 6152 | tf_op jit(solution)/shard_map/ppermute | solution.py:28
  15.3 3.7 collective-permute-start.19
  19.0 1.7 collective-permute-start.20
  20.7 6.3 %collective-permute-start.23 = (f32[128,1]{1,0:T(8,128)S(1)}, f32[128,1]{1,0:T(8,128)S(1)}, u32[]{:S(2)}, u32[]{:S(2)}) collective-permute-start(f32[128,1]{1,0:T(8,128)S(1)} %get-tuple-element.1175), channel_id=1, source_target_pairs={{1,0},{2,1},{3,2},{4,3},{5,4},{6,5},{7,6},{8,7},{9,8},{10,9},{11,1... | collective-permute-start | bytes 1544 | tf_op jit(solution)/shard_map/ppermute | solution.py:28
  56.6 42.2 %copy-start.12 = (f32[64,256]{1,0:T(8,128)}, f32[64,256]{1,0:T(8,128)S(1)}, u32[]{:S(2)}) copy-start(f32[64,256]{1,0:T(8,128)S(1)} %get-tuple-element.1644) | copy-start | bytes 196612 | tf_op jit(solution)/shard_map/while
  56.6 42.2 %copy-start.14 = (f32[64,256]{1,0:T(8,128)}, f32[64,256]{1,0:T(8,128)S(1)}, u32[]{:S(2)}) copy-start(f32[64,256]{1,0:T(8,128)S(1)} %get-tuple-element.1636) | copy-start | bytes 196612 | tf_op jit(solution)/shard_map/while
  56.6 42.2 %copy-start.16 = (f32[64,256]{1,0:T(8,128)}, f32[64,256]{1,0:T(8,128)S(1)}, u32[]{:S(2)}) copy-start(f32[64,256]{1,0:T(8,128)S(1)} %get-tuple-element.1635) | copy-start | bytes 196612 | tf_op jit(solution)/shard_map/while
  56.6 42.4 %copy-start.18 = (f32[64,256]{1,0:T(8,128)}, f32[64,256]{1,0:T(8,128)S(1)}, u32[]{:S(2)}) copy-start(f32[64,256]{1,0:T(8,128)S(1)} %get-tuple-element.1652) | copy-start | bytes 196612 | tf_op jit(solution)/shard_map/while
  56.6 95.5 %copy-start.4 = (f32[64,256]{1,0:T(8,128)}, f32[64,256]{1,0:T(8,128)S(1)}, u32[]{:S(2)}) copy-start(f32[64,256]{1,0:T(8,128)S(1)} %get-tuple-element.1634) | copy-start | bytes 196612 | tf_op jit(solution)/shard_map/while
  56.6 96.7 %copy-start.6 = (f32[64,256]{1,0:T(8,128)}, f32[64,256]{1,0:T(8,128)S(1)}, u32[]{:S(2)}) copy-start(f32[64,256]{1,0:T(8,128)S(1)} %get-tuple-element.1653) | copy-start | bytes 196612 | tf_op jit(solution)/shard_map/while
  56.6 96.7 %copy-start.8 = (f32[64,256]{1,0:T(8,128)}, f32[64,256]{1,0:T(8,128)S(1)}, u32[]{:S(2)}) copy-start(f32[64,256]{1,0:T(8,128)S(1)} %get-tuple-element.1655) | copy-start | bytes 196612 | tf_op jit(solution)/shard_map/while
  56.7 96.7 %copy-start.10 = (f32[64,256]{1,0:T(8,128)}, f32[64,256]{1,0:T(8,128)S(1)}, u32[]{:S(2)}) copy-start(f32[64,256]{1,0:T(8,128)S(1)} %get-tuple-element.1656) | copy-start | bytes 196612 | tf_op jit(solution)/shard_map/while
  56.7 151.3 %copy-start.2 = (f32[64,256]{1,0:T(8,128)}, f32[64,256]{1,0:T(8,128)S(1)}, u32[]{:S(2)}) copy-start(f32[64,256]{1,0:T(8,128)S(1)} %get-tuple-element.1648) | copy-start | bytes 196612 | tf_op jit(solution)/shard_map/while
  56.7 5.1 collective-permute-start
  57.5 6.1 %collective-permute-start.1 = (f32[1,2,512]{2,1,0:T(2,128)S(1)}, f32[1,2,512]{2,1,0:T(2,128)S(1)}, u32[]{:S(2)}, u32[]{:S(2)}) collective-permute-start(f32[1,2,512]{2,1,0:T(2,128)S(1)} %get-tuple-element.1463), channel_id=1, source_target_pairs={{0,16},{16,32},{32,48},{48,64},{64,80},{80,96},{96,112},{112,0},{1... | collective-permute-start | bytes 12296 | tf_op jit(solution)/shard_map/while/body/eval_jaxpr/ppermute | solution.py:45
  59.8 149.5 %copy-start.47 = (pred[256]{0:T(512)(128)(4,1)}, pred[256]{0:T(512)(128)(4,1)S(1)}, u32[]{:S(2)}) copy-start(pred[256]{0:T(512)(128)(4,1)S(1)} %get-tuple-element.1470) | copy-start | bytes 772 | tf_op jit(solution)/shard_map/while
  63.6 23.1 %collective-permute-start.2 = (f32[1,132,2]{2,1,0:T(8,128)S(1)}, f32[1,132,2]{2,1,0:T(8,128)S(1)}, u32[]{:S(2)}, u32[]{:S(2)}) collective-permute-start(f32[1,132,2]{2,1,0:T(8,128)S(1)} %get-tuple-element.1464), channel_id=1, source_target_pairs={{1,0},{2,1},{3,2},{4,3},{5,4},{6,5},{7,6},{8,7},{9,8},{10,9},{11,1... | collective-permute-start | bytes 3176 | tf_op jit(solution)/shard_map/while/body/eval_jaxpr/ppermute | solution.py:48
  66.1 20.6 %collective-permute-start.3 = (f32[1,132,2]{2,1,0:T(8,128)S(1)}, f32[1,132,2]{2,1,0:T(8,128)S(1)}, u32[]{:S(2)}, u32[]{:S(2)}) collective-permute-start(f32[1,132,2]{2,1,0:T(8,128)S(1)} %get-tuple-element.1465), channel_id=1, source_target_pairs={{0,1},{1,2},{2,3},{3,4},{4,5},{5,6},{6,7},{7,8},{8,9},{9,10},{10,1... | collective-permute-start | bytes 3176 | tf_op jit(solution)/shard_map/while/body/eval_jaxpr/ppermute | solution.py:45
  66.1 143.1 %copy-start.49 = (s32[64]{0:T(128)}, s32[64]{0:T(128)S(1)}, u32[]{:S(2)}) copy-start(s32[64]{0:T(128)S(1)} %fusion.559) | copy-start | bytes 772 | tf_op jit(solution)/shard_map/while
  117.6 4.0 collective-permute-start.4
  118.1 6.1 %collective-permute-start.5 = (f32[1,2,512]{2,1,0:T(2,128)S(1)}, f32[1,2,512]{2,1,0:T(2,128)S(1)}, u32[]{:S(2)}, u32[]{:S(2)}) collective-permute-start(f32[1,2,512]{2,1,0:T(2,128)S(1)} %get-tuple-element.1486), channel_id=1, source_target_pairs={{0,16},{16,32},{32,48},{48,64},{64,80},{80,96},{96,112},{112,0},{1... | collective-permute-start | bytes 12296 | tf_op jit(solution)/shard_map/while/body/eval_jaxpr/ppermute | solution.py:45
  124.3 15.6 %collective-permute-start.6 = (f32[1,132,2]{2,1,0:T(8,128)S(1)}, f32[1,132,2]{2,1,0:T(8,128)S(1)}, u32[]{:S(2)}, u32[]{:S(2)}) collective-permute-start(f32[1,132,2]{2,1,0:T(8,128)S(1)} %get-tuple-element.1487), channel_id=1, source_target_pairs={{1,0},{2,1},{3,2},{4,3},{5,4},{6,5},{7,6},{8,7},{9,8},{10,9},{11,1... | collective-permute-start | bytes 3176 | tf_op jit(solution)/shard_map/while/body/eval_jaxpr/ppermute | solution.py:48
  128.9 10.9 %collective-permute-start.7 = (f32[1,132,2]{2,1,0:T(8,128)S(1)}, f32[1,132,2]{2,1,0:T(8,128)S(1)}, u32[]{:S(2)}, u32[]{:S(2)}) collective-permute-start(f32[1,132,2]{2,1,0:T(8,128)S(1)} %get-tuple-element.1488), channel_id=1, source_target_pairs={{0,1},{1,2},{2,3},{3,4},{4,5},{5,6},{6,7},{7,8},{8,9},{9,10},{10,1... | collective-permute-start | bytes 3176 | tf_op jit(solution)/shard_map/while/body/eval_jaxpr/ppermute | solution.py:45
  174.1 4.0 collective-permute-start.8
  174.2 6.1 %collective-permute-start.9 = (f32[1,2,512]{2,1,0:T(2,128)S(1)}, f32[1,2,512]{2,1,0:T(2,128)S(1)}, u32[]{:S(2)}, u32[]{:S(2)}) collective-permute-start(f32[1,2,512]{2,1,0:T(2,128)S(1)} %get-tuple-element.1502), channel_id=1, source_target_pairs={{0,16},{16,32},{32,48},{48,64},{64,80},{80,96},{96,112},{112,0},{1... | collective-permute-start | bytes 12296 | tf_op jit(solution)/shard_map/while/body/eval_jaxpr/ppermute | solution.py:45
  181.0 14.1 %collective-permute-start.10 = (f32[1,132,2]{2,1,0:T(8,128)}, f32[1,132,2]{2,1,0:T(8,128)S(1)}, u32[]{:S(2)}, u32[]{:S(2)}) collective-permute-start(f32[1,132,2]{2,1,0:T(8,128)} %get-tuple-element.1503), channel_id=1, source_target_pairs={{1,0},{2,1},{3,2},{4,3},{5,4},{6,5},{7,6},{8,7},{9,8},{10,9},{11,1... | collective-permute-start | bytes 3176 | tf_op jit(solution)/shard_map/while/body/eval_jaxpr/ppermute | solution.py:48
  184.8 10.3 %collective-permute-start.11 = (f32[1,132,2]{2,1,0:T(8,128)S(1)}, f32[1,132,2]{2,1,0:T(8,128)S(1)}, u32[]{:S(2)}, u32[]{:S(2)}) collective-permute-start(f32[1,132,2]{2,1,0:T(8,128)S(1)} %get-tuple-element.1504), channel_id=1, source_target_pairs={{0,1},{1,2},{2,3},{3,4},{4,5},{5,6},{6,7},{7,8},{8,9},{9,10},{10,1... | collective-permute-start | bytes 3176 | tf_op jit(solution)/shard_map/while/body/eval_jaxpr/ppermute | solution.py:45
  231.6 4.0 collective-permute-start.12
  231.7 6.1 %collective-permute-start.13 = (f32[1,2,512]{2,1,0:T(2,128)S(1)}, f32[1,2,512]{2,1,0:T(2,128)S(1)}, u32[]{:S(2)}, u32[]{:S(2)}) collective-permute-start(f32[1,2,512]{2,1,0:T(2,128)S(1)} %get-tuple-element.1518), channel_id=1, source_target_pairs={{0,16},{16,32},{32,48},{48,64},{64,80},{80,96},{96,112},{112,0},{1... | collective-permute-start | bytes 12296 | tf_op jit(solution)/shard_map/while/body/eval_jaxpr/ppermute | solution.py:45
  238.6 16.8 %collective-permute-start.14 = (f32[1,132,2]{2,1,0:T(8,128)}, f32[1,132,2]{2,1,0:T(8,128)}, u32[]{:S(2)}, u32[]{:S(2)}) collective-permute-start(f32[1,132,2]{2,1,0:T(8,128)} %get-tuple-element.1519), channel_id=1, source_target_pairs={{1,0},{2,1},{3,2},{4,3},{5,4},{6,5},{7,6},{8,7},{9,8},{10,9},{11,1... | collective-permute-start | bytes 3176 | tf_op jit(solution)/shard_map/while/body/eval_jaxpr/ppermute | solution.py:48
  242.5 12.9 %collective-permute-start.15 = (f32[1,132,2]{2,1,0:T(8,128)}, f32[1,132,2]{2,1,0:T(8,128)}, u32[]{:S(2)}, u32[]{:S(2)}) collective-permute-start(f32[1,132,2]{2,1,0:T(8,128)} %get-tuple-element.1520), channel_id=1, source_target_pairs={{0,1},{1,2},{2,3},{3,4},{4,5},{5,6},{6,7},{7,8},{8,9},{9,10},{10,1... | collective-permute-start | bytes 3176 | tf_op jit(solution)/shard_map/while/body/eval_jaxpr/ppermute | solution.py:45
  260.7 19.1 %copy-start.24 = (f32[1,64,256]{2,1,0:T(8,128)S(1)}, f32[1,64,256]{2,1,0:T(8,128)}, u32[]{:S(2)}) copy-start(f32[1,64,256]{2,1,0:T(8,128)} %slice.1705) | copy-start | bytes 196612 | tf_op jit(solution)/shard_map/while
  302.9 43.0 %copy-start.12 = (f32[64,256]{1,0:T(8,128)}, f32[64,256]{1,0:T(8,128)S(1)}, u32[]{:S(2)}) copy-start(f32[64,256]{1,0:T(8,128)S(1)} %get-tuple-element.1644) | copy-start | bytes 196612 | tf_op jit(solution)/shard_map/while
  302.9 43.0 %copy-start.14 = (f32[64,256]{1,0:T(8,128)}, f32[64,256]{1,0:T(8,128)S(1)}, u32[]{:S(2)}) copy-start(f32[64,256]{1,0:T(8,128)S(1)} %get-tuple-element.1636) | copy-start | bytes 196612 | tf_op jit(solution)/shard_map/while
  302.9 43.0 %copy-start.16 = (f32[64,256]{1,0:T(8,128)}, f32[64,256]{1,0:T(8,128)S(1)}, u32[]{:S(2)}) copy-start(f32[64,256]{1,0:T(8,128)S(1)} %get-tuple-element.1635) | copy-start | bytes 196612 | tf_op jit(solution)/shard_map/while
  302.9 43.2 %copy-start.18 = (f32[64,256]{1,0:T(8,128)}, f32[64,256]{1,0:T(8,128)S(1)}, u32[]{:S(2)}) copy-start(f32[64,256]{1,0:T(8,128)S(1)} %get-tuple-element.1652) | copy-start | bytes 196612 | tf_op jit(solution)/shard_map/while
  302.9 96.4 %copy-start.4 = (f32[64,256]{1,0:T(8,128)}, f32[64,256]{1,0:T(8,128)S(1)}, u32[]{:S(2)}) copy-start(f32[64,256]{1,0:T(8,128)S(1)} %get-tuple-element.1634) | copy-start | bytes 196612 | tf_op jit(solution)/shard_map/while
  302.9 97.6 %copy-start.6 = (f32[64,256]{1,0:T(8,128)}, f32[64,256]{1,0:T(8,128)S(1)}, u32[]{:S(2)}) copy-start(f32[64,256]{1,0:T(8,128)S(1)} %get-tuple-element.1653) | copy-start | bytes 196612 | tf_op jit(solution)/shard_map/while
  303.0 97.6 %copy-start.8 = (f32[64,256]{1,0:T(8,128)}, f32[64,256]{1,0:T(8,128)S(1)}, u32[]{:S(2)}) copy-start(f32[64,256]{1,0:T(8,128)S(1)} %get-tuple-element.1655) | copy-start | bytes 196612 | tf_op jit(solution)/shard_map/while
  303.0 97.6 %copy-start.10 = (f32[64,256]{1,0:T(8,128)}, f32[64,256]{1,0:T(8,128)S(1)}, u32[]{:S(2)}) copy-start(f32[64,256]{1,0:T(8,128)S(1)} %get-tuple-element.1656) | copy-start | bytes 196612 | tf_op jit(solution)/shard_map/while
  303.0 152.2 %copy-start.2 = (f32[64,256]{1,0:T(8,128)}, f32[64,256]{1,0:T(8,128)S(1)}, u32[]{:S(2)}) copy-start(f32[64,256]{1,0:T(8,128)S(1)} %get-tuple-element.1648) | copy-start | bytes 196612 | tf_op jit(solution)/shard_map/while
  303.0 5.1 collective-permute-start
  303.1 6.1 %collective-permute-start.1 = (f32[1,2,512]{2,1,0:T(2,128)S(1)}, f32[1,2,512]{2,1,0:T(2,128)S(1)}, u32[]{:S(2)}, u32[]{:S(2)}) collective-permute-start(f32[1,2,512]{2,1,0:T(2,128)S(1)} %get-tuple-element.1463), channel_id=1, source_target_pairs={{0,16},{16,32},{32,48},{48,64},{64,80},{80,96},{96,112},{112,0},{1... | collective-permute-start | bytes 12296 | tf_op jit(solution)/shard_map/while/body/eval_jaxpr/ppermute | solution.py:45
  306.1 150.5 %copy-start.47 = (pred[256]{0:T(512)(128)(4,1)}, pred[256]{0:T(512)(128)(4,1)S(1)}, u32[]{:S(2)}) copy-start(pred[256]{0:T(512)(128)(4,1)S(1)} %get-tuple-element.1470) | copy-start | bytes 772 | tf_op jit(solution)/shard_map/while
  309.3 24.6 %collective-permute-start.2 = (f32[1,132,2]{2,1,0:T(8,128)S(1)}, f32[1,132,2]{2,1,0:T(8,128)S(1)}, u32[]{:S(2)}, u32[]{:S(2)}) collective-permute-start(f32[1,132,2]{2,1,0:T(8,128)S(1)} %get-tuple-element.1464), channel_id=1, source_target_pairs={{1,0},{2,1},{3,2},{4,3},{5,4},{6,5},{7,6},{8,7},{9,8},{10,9},{11,1... | collective-permute-start | bytes 3176 | tf_op jit(solution)/shard_map/while/body/eval_jaxpr/ppermute | solution.py:48
  313.3 20.6 %collective-permute-start.3 = (f32[1,132,2]{2,1,0:T(8,128)S(1)}, f32[1,132,2]{2,1,0:T(8,128)S(1)}, u32[]{:S(2)}, u32[]{:S(2)}) collective-permute-start(f32[1,132,2]{2,1,0:T(8,128)S(1)} %get-tuple-element.1465), channel_id=1, source_target_pairs={{0,1},{1,2},{2,3},{3,4},{4,5},{5,6},{6,7},{7,8},{8,9},{9,10},{10,1... | collective-permute-start | bytes 3176 | tf_op jit(solution)/shard_map/while/body/eval_jaxpr/ppermute | solution.py:45
  313.3 143.2 %copy-start.49 = (s32[64]{0:T(128)}, s32[64]{0:T(128)S(1)}, u32[]{:S(2)}) copy-start(s32[64]{0:T(128)S(1)} %fusion.559) | copy-start | bytes 772 | tf_op jit(solution)/shard_map/while
  364.8 4.0 collective-permute-start.4
  365.1 6.1 %collective-permute-start.5 = (f32[1,2,512]{2,1,0:T(2,128)S(1)}, f32[1,2,512]{2,1,0:T(2,128)S(1)}, u32[]{:S(2)}, u32[]{:S(2)}) collective-permute-start(f32[1,2,512]{2,1,0:T(2,128)S(1)} %get-tuple-element.1486), channel_id=1, source_target_pairs={{0,16},{16,32},{32,48},{48,64},{64,80},{80,96},{96,112},{112,0},{1... | collective-permute-start | bytes 12296 | tf_op jit(solution)/shard_map/while/body/eval_jaxpr/ppermute | solution.py:45
  371.2 15.9 %collective-permute-start.6 = (f32[1,132,2]{2,1,0:T(8,128)S(1)}, f32[1,132,2]{2,1,0:T(8,128)S(1)}, u32[]{:S(2)}, u32[]{:S(2)}) collective-permute-start(f32[1,132,2]{2,1,0:T(8,128)S(1)} %get-tuple-element.1487), channel_id=1, source_target_pairs={{1,0},{2,1},{3,2},{4,3},{5,4},{6,5},{7,6},{8,7},{9,8},{10,9},{11,1... | collective-permute-start | bytes 3176 | tf_op jit(solution)/shard_map/while/body/eval_jaxpr/ppermute | solution.py:48
  376.2 10.9 %collective-permute-start.7 = (f32[1,132,2]{2,1,0:T(8,128)S(1)}, f32[1,132,2]{2,1,0:T(8,128)S(1)}, u32[]{:S(2)}, u32[]{:S(2)}) collective-permute-start(f32[1,132,2]{2,1,0:T(8,128)S(1)} %get-tuple-element.1488), channel_id=1, source_target_pairs={{0,1},{1,2},{2,3},{3,4},{4,5},{5,6},{6,7},{7,8},{8,9},{9,10},{10,1... | collective-permute-start | bytes 3176 | tf_op jit(solution)/shard_map/while/body/eval_jaxpr/ppermute | solution.py:45
  421.4 4.0 collective-permute-start.8
  421.5 6.1 %collective-permute-start.9 = (f32[1,2,512]{2,1,0:T(2,128)S(1)}, f32[1,2,512]{2,1,0:T(2,128)S(1)}, u32[]{:S(2)}, u32[]{:S(2)}) collective-permute-start(f32[1,2,512]{2,1,0:T(2,128)S(1)} %get-tuple-element.1502), channel_id=1, source_target_pairs={{0,16},{16,32},{32,48},{48,64},{64,80},{80,96},{96,112},{112,0},{1... | collective-permute-start | bytes 12296 | tf_op jit(solution)/shard_map/while/body/eval_jaxpr/ppermute | solution.py:45
  428.3 14.1 %collective-permute-start.10 = (f32[1,132,2]{2,1,0:T(8,128)}, f32[1,132,2]{2,1,0:T(8,128)S(1)}, u32[]{:S(2)}, u32[]{:S(2)}) collective-permute-start(f32[1,132,2]{2,1,0:T(8,128)} %get-tuple-element.1503), channel_id=1, source_target_pairs={{1,0},{2,1},{3,2},{4,3},{5,4},{6,5},{7,6},{8,7},{9,8},{10,9},{11,1... | collective-permute-start | bytes 3176 | tf_op jit(solution)/shard_map/while/body/eval_jaxpr/ppermute | solution.py:48
  432.0 10.3 %collective-permute-start.11 = (f32[1,132,2]{2,1,0:T(8,128)S(1)}, f32[1,132,2]{2,1,0:T(8,128)S(1)}, u32[]{:S(2)}, u32[]{:S(2)}) collective-permute-start(f32[1,132,2]{2,1,0:T(8,128)S(1)} %get-tuple-element.1504), channel_id=1, source_target_pairs={{0,1},{1,2},{2,3},{3,4},{4,5},{5,6},{6,7},{7,8},{8,9},{9,10},{10,1... | collective-permute-start | bytes 3176 | tf_op jit(solution)/shard_map/while/body/eval_jaxpr/ppermute | solution.py:45
  478.9 4.0 collective-permute-start.12
  479.0 6.1 %collective-permute-start.13 = (f32[1,2,512]{2,1,0:T(2,128)S(1)}, f32[1,2,512]{2,1,0:T(2,128)S(1)}, u32[]{:S(2)}, u32[]{:S(2)}) collective-permute-start(f32[1,2,512]{2,1,0:T(2,128)S(1)} %get-tuple-element.1518), channel_id=1, source_target_pairs={{0,16},{16,32},{32,48},{48,64},{64,80},{80,96},{96,112},{112,0},{1... | collective-permute-start | bytes 12296 | tf_op jit(solution)/shard_map/while/body/eval_jaxpr/ppermute | solution.py:45
  485.8 16.8 %collective-permute-start.14 = (f32[1,132,2]{2,1,0:T(8,128)}, f32[1,132,2]{2,1,0:T(8,128)}, u32[]{:S(2)}, u32[]{:S(2)}) collective-permute-start(f32[1,132,2]{2,1,0:T(8,128)} %get-tuple-element.1519), channel_id=1, source_target_pairs={{1,0},{2,1},{3,2},{4,3},{5,4},{6,5},{7,6},{8,7},{9,8},{10,9},{11,1... | collective-permute-start | bytes 3176 | tf_op jit(solution)/shard_map/while/body/eval_jaxpr/ppermute | solution.py:48
  489.8 12.9 %collective-permute-start.15 = (f32[1,132,2]{2,1,0:T(8,128)}, f32[1,132,2]{2,1,0:T(8,128)}, u32[]{:S(2)}, u32[]{:S(2)}) collective-permute-start(f32[1,132,2]{2,1,0:T(8,128)} %get-tuple-element.1520), channel_id=1, source_target_pairs={{0,1},{1,2},{2,3},{3,4},{4,5},{5,6},{6,7},{7,8},{8,9},{9,10},{10,1... | collective-permute-start | bytes 3176 | tf_op jit(solution)/shard_map/while/body/eval_jaxpr/ppermute | solution.py:45
  551.3 33.5 %copy-start = (f32[1,128,512]{2,1,0:T(8,128)}, f32[1,128,512]{2,1,0:T(8,128)S(1)}, u32[]{:S(2)}) copy-start(f32[1,128,512]{2,1,0:T(8,128)S(1)} %get-tuple-element.1730) | copy-start | bytes 786436
  (83 other events, 349.3 us)
where the time goes:
time: 590 us; the launch traced here: 585 us
  local copies, waits for them, and re-layouts  348 us (59%)
  other arithmetic  96.1 us (16%)
  starting transfers between devices  75.3 us (13%)
  blocking collectives  32.3 us (5%)
  waiting for transfers between devices  28.8 us (5%)
    slice x84, local copies, waits for them, and re-layouts, corners(): source[..., first_index::2, second_index::2]  224 us
    pad x32, local copies, waits for them, and re-layouts, join_corners(): padded = lax.pad(piece, jnp.zeros((), piece.dtype), config)  103 us
    select_n x16, other arithmetic, one_sweep(): jnp.where(chosen, updated[corner], before[corner])  39.6 us
    ppermute x16, starting transfers between devices, with_halo(): lax.ppermute(lax.slice_in_dim(block, 0, width, axis=dim), axis, backward)  33.4 us
    psum x5, blocking collectives, one_axis_at_a_time(): shard = lax.psum(shard, axis)  32.3 us
    ppermute x16, starting transfers between devices, with_halo(): lax.ppermute(lax.slice_in_dim(block, block.shape[dim] - width, None, axis...  23 us
    ppermute x16, waiting for transfers between devices, with_halo(): lax.ppermute(lax.slice_in_dim(block, block.shape[dim] - width, None, axis...  16.5 us
    another operation x10, other arithmetic  16.2 us
  transfers between devices with their start and end apart: 40, of which 17 were waited for; matrix products, arithmetic and copies ran while one was open for 19% of the time, Pallas kernels for 0%

commit v1 on v0

v1 whole, which is shorter than its diff:
```python
import jax
import jax.numpy as jnp
from jax import lax
from jax.experimental import pallas as pl
from jax.experimental.pallas import tpu as pltpu
from jax.sharding import PartitionSpec as P

MESH = pl.DeviceIdType.MESH
SWEEPS = 2
COLOURS = 4
PHASES = SWEEPS * COLOURS
HALO = 16
TR = 128
TC = 512
EXT = TR + 2 * HALO
ROWS = EXT // 4
GROUPS = ROWS // 8
PAD = 8
PADDED = ROWS + 2 * PAD
LANES = 128
MIX = 73244475
STEP = 1.0 / 8388608.0
NODES = 8388608.0
NEIGHBOURS = [(a, b) for a in (-1, 0, 1) for b in (-1, 0, 1) if (a, b) != (0, 0)]
LOWER = {(1, 0): 4, (2, 0): 5, (2, 1): 6, (3, 0): 7, (3, 1): 8, (3, 2): 9}
SINE = (6.283185307179586, -41.34170224039976, 81.60524927607506, -76.70585975306136, 42.05869394489765, -15.09464257682298, 3.8199525848482803)


def tile():
    return lax.broadcasted_iota(jnp.int32, (8, LANES), 0), lax.broadcasted_iota(jnp.int32, (8, LANES), 1)


def logical(value, amount):
    return lax.shift_right_logical(value, jnp.full_like(value, amount))


def scramble(hashed):
    hashed = (hashed ^ logical(hashed, 16)) * MIX
    hashed = (hashed ^ logical(hashed, 16)) * MIX
    return hashed ^ logical(hashed, 16)


def gaussian(base):
    one = (logical(scramble(base), 9).astype(jnp.float32) + 1.0) * STEP
    two = logical(scramble(base + 1), 9).astype(jnp.float32) * STEP
    squared = -2.0 * jnp.log(one)
    radius = squared * lax.rsqrt(jnp.maximum(squared, 1e-30))
    turn = jnp.abs(two - 0.5) - 0.25
    square = turn * turn
    series = jnp.full_like(square, SINE[6])
    for n in range(5, -1, -1):
        series = series * square + SINE[n]
    return radius * (turn * series)


def lane_next(main, side, lane):
    main, side = pltpu.roll(main, LANES - 1, 1), pltpu.roll(side, LANES - 1, 1)
    last = lane == LANES - 1
    return jnp.where(last, side, main), jnp.where(last, main, side)


def lane_prev(main, side, lane):
    main, side = pltpu.roll(main, 1, 1), pltpu.roll(side, 1, 1)
    first = lane == 0
    return jnp.where(first, side, main), jnp.where(first, main, side)


def pick(index, lane_source):
    return jnp.take_along_axis(lane_source, index, axis=1, mode="promise_in_bounds")


def kernel(
    field_ref, info_ref, kappa_ref, mass_ref, seed_ref, order_ref, out_ref, energy_ref,
    nat, pack, strip_l, strip_r, seedbuf, seedmap, noise, fld, stf, inf, inv, scl, kd, fac, delta, acc, outn, e1, e2,
    load_sem, send_sem, recv_sem, store_sem, esend, erecv,
):
    r, c = lax.axis_index("row"), lax.axis_index("col")
    sub, lane = tile()

    def at(dr, dc):
        return (lax.rem(r + (dr + 8), 8), lax.rem(c + (dc + 16), 16))

    barrier = pltpu.get_barrier_semaphore()
    peers = [at(0, k) for k in range(1, 16)] + [at(k, 0) for k in range(1, 8)]
    peers += [at(a, b) for a in (-1, 1) for b in (-1, 1)]
    for peer in peers:
        pl.semaphore_signal(barrier, inc=1, device_id=peer, device_id_type=MESH)

    sources = (field_ref.at[0], info_ref, kappa_ref, mass_ref)
    loads = []
    for i in range(4):
        for k in range(4):
            loads.append(
                pltpu.make_async_copy(
                    sources[i].at[:, pl.ds(LANES * k, LANES)], nat.at[i, k, pl.ds(HALO, TR)], load_sem.at[i, k]
                )
            )
            loads[-1].start()

    own = jnp.zeros((8, LANES), jnp.int32)
    for t in range(SWEEPS):
        for colour in range(COLOURS):
            seed = jnp.int32(0)
            for k in range(COLOURS):
                seed = seed + jnp.where(order_ref[k] == colour, seed_ref[t * COLOURS + k], 0)
            own = jnp.where(sub == t * COLOURS + colour, seed, own)
    seedbuf[4] = own

    for load in loads:
        load.wait()

    def pack_rows(g, _):
        rows = pl.ds(HALO + 8 * g, 8)
        total = jnp.zeros((8, LANES), jnp.float32)
        for i in range(4):
            right = pltpu.roll(nat[i, 3, rows, :], 16 * i + 16, 1)
            left = pltpu.roll(nat[i, 0, rows, :], 64 + 16 * i, 1)
            total = jnp.where((lane >= 16 * i) & (lane < 16 * i + 16), right, total)
            total = jnp.where((lane >= 64 + 16 * i) & (lane < 80 + 16 * i), left, total)
        pack[pl.ds(8 * g, 8), :] = total
        return 0

    lax.fori_loop(0, TR // 8, pack_rows, 0)

    pl.semaphore_wait(barrier, len(peers))
    copies = []

    def send(source, target, where):
        n = len(copies)
        copies.append(
            pltpu.make_async_remote_copy(
                src_ref=source,
                dst_ref=target,
                send_sem=send_sem.at[n],
                recv_sem=recv_sem.at[n],
                device_id=at(*where),
                device_id_type=MESH,
            )
        )
        copies[-1].start()

    for dr, dc in NEIGHBOURS:
        send(seedbuf.at[4], seedbuf.at[(1 - dr) * 3 + 1 - dc], (dr, dc))
    for dr in (-1, 0, 1):
        mine = {-1: pl.ds(0, HALO), 0: pl.ds(0, TR), 1: pl.ds(TR - HALO, HALO)}[dr]
        theirs = {-1: pl.ds(HALO + TR, HALO), 0: pl.ds(HALO, TR), 1: pl.ds(0, HALO)}[dr]
        send(pack.at[mine], strip_l.at[theirs], (dr, 1))
        send(pack.at[mine], strip_r.at[theirs], (dr, -1))
    send(nat.at[:, :, pl.ds(HALO, HALO)], nat.at[:, :, pl.ds(HALO + TR, HALO)], (-1, 0))
    send(nat.at[:, :, pl.ds(TR, HALO)], nat.at[:, :, pl.ds(0, HALO)], (1, 0))

    zero = jnp.zeros((8, LANES), jnp.float32)

    def clear(n, _):
        for v in range(2):
            for buffer in (fld, inv, scl, kd):
                buffer[n, v, 0:PAD, :] = zero
                buffer[n, v, PAD + ROWS : PADDED, :] = zero
            for g in range(GROUPS):
                kd[n, v, PAD + 8 * g : PAD + 8 * g + 8, :] = zero
        return 0

    lax.fori_loop(0, 16, clear, 0)

    def draw(g, group_class, v):
        for rho in range(4):
            row = 4 * ((sub + (8 * g + 28)) & 31) + rho
            for kappa in range(4):
                colour = 2 * (rho // 2) + kappa // 2
                offset = 2 * (row * TC + 4 * lane + kappa)
                for t in range(SWEEPS):
                    seeds = seedmap[t * COLOURS + colour, v, group_class]
                    noise[t, 4 * rho + kappa, v, pl.ds(pl.multiple_of(8 * g, 8), 8), :] = gaussian(seeds + offset)

    def splat(slot, n):
        return jnp.broadcast_to(seedbuf[slot, n : n + 1, :], (8, LANES))

    for n in range(8):
        seedmap[n, 0, 1] = splat(4, n)

    def inner(g, _):
        draw(g, 1, 0)
        return 0

    lax.fori_loop(1, GROUPS - 1, inner, 0)

    for copy in copies[:8]:
        copy.wait()
    for n in range(8):
        seedmap[n, 0, 0] = jnp.where(sub < 4, splat(1, n), splat(4, n))
        seedmap[n, 0, 2] = jnp.where(sub < 4, splat(4, n), splat(7, n))
        rows = [jnp.where(lane < 64, splat(3 * a + 2, n), splat(3 * a, n)) for a in range(3)]
        seedmap[n, 1, 0] = jnp.where(sub < 4, rows[0], rows[1])
        seedmap[n, 1, 1] = rows[1]
        seedmap[n, 1, 2] = jnp.where(sub < 4, rows[1], rows[2])
    draw(0, 0, 0)
    draw(GROUPS - 1, 2, 0)

    def side(g, _):
        draw(g, jnp.where(g == 0, 0, jnp.where(g == GROUPS - 1, 2, 1)), 1)
        return 0

    lax.fori_loop(0, GROUPS, side, 0)

    for copy in copies[8:]:
        copy.wait()

    block = lane // 32
    split = [4 * (lane & 31) + ((block - k) & 3) for k in range(4)]
    edge = lane < 64
    used = (lane < 4) | (lane >= 124)

    def planes(g, _):
        rows = pl.ds(pl.multiple_of(8 * g, 8), 8)
        padded = pl.ds(pl.multiple_of(8 * g + PAD, 8), 8)
        for rho in range(4):
            natural = pl.ds(32 * g + rho, 8, stride=4)
            mixed = jnp.where(edge, strip_l[natural, :], strip_r[natural, :])
            values = []
            for i in range(4):
                chunks = [pick(split[k], nat[i, k, natural, :]) for k in range(4)]
                row = []
                for kappa in range(4):
                    m = chunks[(-kappa) & 3]
                    for b in range(1, 4):
                        m = jnp.where(block == b, chunks[(b - kappa) & 3], m)
                    main = pltpu.roll(m, (LANES - 32 * kappa) % LANES, 1) if kappa else m
                    index = jnp.where(edge, 64 + 16 * i + 4 * (lane & 3) + kappa, 16 * i + 4 * (lane & 3) + kappa)
                    filler = 0.0 if i < 2 else 1.0
                    row.append((main, jnp.where(used, pick(index, mixed), filler)))
                values.append(row)
            for kappa in range(4):
                n = 4 * rho + kappa
                for v in range(2):
                    mass = values[3][kappa][v]
                    fld[n, v, padded, :] = values[0][kappa][v]
                    inf[n, v, rows, :] = values[1][kappa][v]
                    stf[n, v, rows, :] = values[2][kappa][v] * mass + 4.0
                    inv[n, v, padded, :] = 1.0 / mass
        return 0

    lax.fori_loop(0, GROUPS, planes, 0)

    def around(ref, rho, kappa, base):
        up = (4 * ((rho + 3) % 4) + kappa, base - 1 if rho == 0 else base)
        down = (4 * ((rho + 1) % 4) + kappa, base + 1 if rho == 3 else base)
        here = pl.ds(base, 8)
        left = [ref[4 * rho + (kappa + 3) % 4, v, here, :] for v in range(2)]
        right = [ref[4 * rho + (kappa + 1) % 4, v, here, :] for v in range(2)]
        if kappa == 0:
            left = lane_prev(*left, lane)
        if kappa == 3:
            right = lane_next(*right, lane)
        return [
            ref[up[0], v, pl.ds(up[1], 8), :] + ref[down[0], v, pl.ds(down[1], 8), :] + left[v] + right[v]
            for v in range(2)
        ]

    def is_own(g):
        j = sub + 8 * g
        return (j >= 4) & (j < 36)

    def first(g, total):
        base = pl.multiple_of(8 * g + PAD, 8)
        rows = pl.ds(pl.multiple_of(8 * g, 8), 8)
        here = pl.ds(base, 8)
        part = zero
        for rho in range(4):
            for kappa in range(4):
                n = 4 * rho + kappa
                near = around(fld, rho, kappa, base)
                for v in range(2):
                    value = fld[n, v, here, :]
                    applied = stf[n, v, rows, :] * value - near[v]
                    scaled = inv[n, v, here, :] * applied
                    scl[n, v, here, :] = scaled
                    if v == 0:
                        part = part + (0.5 * scaled * applied - inf[n, v, rows, :] * value)
        return total + jnp.where(is_own(g), part, 0.0)

    acc[0] = lax.fori_loop(0, GROUPS, first, zero)

    def factors(g, _):
        base = pl.multiple_of(8 * g + PAD, 8)
        rows = pl.ds(pl.multiple_of(8 * g, 8), 8)
        here = pl.ds(base, 8)
        for colour in range(COLOURS):
            top, left = 2 * (colour // 2), 2 * (colour % 2)
            corner = [(top + n // 2, left + n % 2) for n in range(4)]
            near = [around(inv, rho, kappa, base) for rho, kappa in corner]
            for v in range(2):
                s = [stf[4 * rho + kappa, v, rows, :] for rho, kappa in corner]
                w = [inv[4 * rho + kappa, v, here, :] for rho, kappa in corner]
                sw = [s[n] * w[n] for n in range(4)]
                q = {(n, n): s[n] * sw[n] + near[n][v] for n in range(4)}
                for a, b in ((1, 0), (2, 0), (3, 1), (3, 2)):
                    q[a, b] = -(sw[a] + sw[b])
                q[3, 0] = w[1] + w[2]
                q[2, 1] = w[0] + w[3]
                low = {}
                for a in range(4):
                    for b in range(a + 1):
                        running = q[a, b]
                        for m in range(b):
                            running = running - low[a, m] * low[b, m]
                        low[a, b] = lax.rsqrt(running) if a == b else running * low[b, b]
                for n in range(4):
                    fac[n, colour, v, rows, :] = low[n, n]
                for (a, b), n in LOWER.items():
                    fac[n, colour, v, rows, :] = low[a, b]
        return 0

    lax.fori_loop(0, GROUPS, factors, 0)

    def resample(i, g, total, scatter):
        t, k = i // COLOURS, lax.rem(i, COLOURS)
        colour = order_ref[k]
        a, b = lax.shift_right_logical(colour, 1), colour & 1
        low_b = jnp.full((8, LANES), b, jnp.int32) == 0
        base = pl.multiple_of(8 * g + PAD, 8)
        rows = pl.ds(pl.multiple_of(8 * g, 8), 8)
        here = pl.ds(base, 8)
        rel_row = [2 * a, 2 * a + 1, (2 * a + 2) & 3, (2 * a + 3) & 3]
        rel_col = [2 * b, 2 * b + 1, (2 * b + 2) & 3, (2 * b + 3) & 3]
        above = pl.ds(base - jnp.where(a == 0, 1, 0), 8)
        below = pl.ds(base + jnp.where(a == 1, 1, 0), 8)

        def read(p, q, where=here):
            return [scl[4 * rel_row[p] + rel_col[q], v, where, :] for v in range(2)]

        node = [[read(p, q) for q in range(2)] for p in range(2)]
        up = [read(3, q, above) for q in range(2)]
        down = [read(2, q, below) for q in range(2)]
        left, right = [], []
        for p in range(2):
            raw = read(p, 3)
            moved = lane_prev(*raw, lane)
            left.append([jnp.where(low_b, moved[v], raw[v]) for v in range(2)])
            raw = read(p, 2)
            moved = lane_next(*raw, lane)
            right.append([jnp.where(low_b, raw[v], moved[v]) for v in range(2)])
        moves = []
        for v in range(2):
            f, drawn = [], []
            inverse = [fac[n, colour, v, rows, :] for n in range(4)]
            low = {key: fac[n, colour, v, rows, :] for key, n in LOWER.items()}
            for n in range(4):
                p, q = n // 2, n % 2
                place = 4 * rel_row[p] + rel_col[q]
                near = node[1 - p][q][v] + node[p][1 - q][v]
                near = near + (down if p else up)[q][v] + (right if q else left)[p][v]
                running = inf[place, v, rows, :] - stf[place, v, rows, :] * node[p][q][v] + near
                for m in range(n):
                    running = running - low[n, m] * f[m]
                f.append(running * inverse[n])
                drawn.append(noise[t, place, v, rows, :])
            target = [f[n] + drawn[n] for n in range(4)]
            if v == 0 and scatter:
                part = (drawn[0] - f[0]) * target[0]
                for n in range(1, 4):
                    part = part + (drawn[n] - f[n]) * target[n]
                total = total + jnp.where(is_own(g), 0.5 * part, 0.0)
            move = [None] * 4
            for n in reversed(range(4)):
                running = target[n]
                for m in range(n + 1, 4):
                    running = running - low[m, n] * move[m]
                move[n] = running * inverse[n]
                if v == 0:
                    delta[i, n, rows, :] = move[n]
            if scatter:
                for n in range(4):
                    p, q = n // 2, n % 2
                    place = 4 * rel_row[p] + rel_col[q]
                    kd[4 * p + q, v, here, :] = move[n ^ 1] + move[n ^ 2] - stf[place, v, rows, :] * move[n]
                for q in range(2):
                    kd[12 + q, v, here, :] = move[q]
                    kd[8 + q, v, here, :] = move[2 + q]
            moves.append(move)
        if scatter:
            for p in range(2):
                raw = [moves[v][2 * p] for v in range(2)]
                moved = lane_next(*raw, lane)
                for v in range(2):
                    kd[4 * p + 3, v, here, :] = jnp.where(low_b, moved[v], raw[v])
                raw = [moves[v][2 * p + 1] for v in range(2)]
                moved = lane_prev(*raw, lane)
                for v in range(2):
                    kd[4 * p + 2, v, here, :] = jnp.where(low_b, raw[v], moved[v])
        return total

    def spread(i, g):
        colour = order_ref[lax.rem(i, COLOURS)]
        a, b = lax.shift_right_logical(colour, 1), colour & 1
        base = pl.multiple_of(8 * g + PAD, 8)
        here = pl.ds(base, 8)
        for rho in range(4):
            where = here
            if rho == 3:
                where = pl.ds(base + jnp.where(a == 0, 1, 0), 8)
            if rho == 0:
                where = pl.ds(base - jnp.where(a == 1, 1, 0), 8)
            for kappa in range(4):
                n = 4 * rho + kappa
                place = 4 * ((rho + 4 - 2 * a) & 3) + ((kappa + 4 - 2 * b) & 3)
                for v in range(2):
                    scl[n, v, here, :] = scl[n, v, here, :] - inv[n, v, here, :] * kd[place, v, where, :]

    def phase(i, _):
        acc[i + 1] = lax.fori_loop(0, GROUPS, lambda g, total: resample(i, g, total, True), zero)
        lax.fori_loop(0, GROUPS, lambda g, _: (spread(i, g), 0)[1], 0)
        return 0

    lax.fori_loop(0, PHASES - 1, phase, 0)

    line = jnp.zeros((1, LANES), jnp.float32)
    for k in range(PHASES):
        change = jnp.sum(jnp.sum(acc[k], axis=0, keepdims=True), axis=1, keepdims=True)
        line = line + jnp.where(lane[0:1] >= k, change, 0.0)
    e1[pl.ds(c, 1), :] = line
    for k in range(1, 16):
        pltpu.make_async_remote_copy(
            src_ref=e1.at[pl.ds(c, 1)], dst_ref=e1.at[pl.ds(c, 1)], send_sem=esend.at[0], recv_sem=erecv.at[0],
            device_id=at(0, k), device_id_type=MESH,
        ).start()

    lax.fori_loop(0, GROUPS, lambda g, total: resample(PHASES - 1, g, total, False), zero)

    turn_of = []
    for colour in range(COLOURS):
        turn = jnp.int32(0)
        for k in range(COLOURS):
            turn = jnp.where(order_ref[k] == colour, jnp.int32(k), turn)
        turn_of.append(turn)
    merge = [32 * (((lane & 3) + k) & 3) + lane // 4 for k in range(4)]

    def natural_rows(h, _):
        for rho in range(4):
            shifted = []
            for kappa in range(4):
                turn = turn_of[2 * (rho // 2) + kappa // 2]
                n = 2 * (rho % 2) + kappa % 2
                value = fld[4 * rho + kappa, 0, pl.ds(8 * h + PAD + 4, 8), :]
                value = value + delta[turn, n, pl.ds(8 * h + 4, 8), :]
                value = value + delta[turn + COLOURS, n, pl.ds(8 * h + 4, 8), :]
                shifted.append(pltpu.roll(value, 32 * kappa, 1) if kappa else value)
            for k in range(4):
                m = shifted[(-k) & 3]
                for b in range(1, 4):
                    m = jnp.where(block == b, shifted[(b - k) & 3], m)
                outn[k, pl.ds(32 * h + rho, 8, stride=4), :] = pick(merge[k], m)
        return 0

    lax.fori_loop(0, 4, natural_rows, 0)
    stores = [
        pltpu.make_async_copy(outn.at[k], out_ref.at[0, :, pl.ds(LANES * k, LANES)], store_sem.at[k]) for k in range(4)
    ]
    for store in stores:
        store.start()

    def finish(buffer, count, sem, where):
        pltpu.make_async_remote_copy(
            src_ref=buffer.at[pl.ds(0, count)], dst_ref=buffer.at[pl.ds(0, count)], send_sem=esend.at[sem],
            recv_sem=erecv.at[sem], device_id=where, device_id_type=MESH,
        ).wait()

    finish(e1, 15, 0, at(0, 1))
    e2[pl.ds(r, 1), :] = jnp.sum(e1[...], axis=0, keepdims=True)
    for k in range(1, 8):
        pltpu.make_async_remote_copy(
            src_ref=e2.at[pl.ds(r, 1)], dst_ref=e2.at[pl.ds(r, 1)], send_sem=esend.at[1], recv_sem=erecv.at[1],
            device_id=at(k, 0), device_id_type=MESH,
        ).start()
    finish(e2, 7, 1, at(1, 0))
    energy_ref[...] = jnp.broadcast_to(jnp.sum(e2[...], axis=0, keepdims=True) * (1.0 / NODES), (8, LANES))
    for store in stores:
        store.wait()


def local(initial_field, information, kappa_squared, lumped_mass, noise_seeds, colour_order):
    f32, i32 = jnp.float32, jnp.int32
    anywhere = pl.BlockSpec(memory_space=pl.ANY)
    scalar = pl.BlockSpec(memory_space=pltpu.SMEM)
    dma = pltpu.SemaphoreType.DMA
    final_field, energies = pl.pallas_call(
        kernel,
        out_shape=(jax.ShapeDtypeStruct((1, TR, TC), f32), jax.ShapeDtypeStruct((8, LANES), f32)),
        in_specs=[anywhere] * 4 + [scalar] * 2,
        out_specs=(anywhere, pl.BlockSpec(memory_space=pltpu.VMEM)),
        scratch_shapes=[
            pltpu.VMEM((4, 4, EXT, LANES), f32),
            pltpu.VMEM((TR, LANES), f32),
            pltpu.VMEM((EXT, LANES), f32),
            pltpu.VMEM((EXT, LANES), f32),
            pltpu.VMEM((9, 8, LANES), i32),
            pltpu.VMEM((8, 2, 3, 8, LANES), i32),
            pltpu.VMEM((SWEEPS, 16, 2, ROWS, LANES), f32),
            pltpu.VMEM((16, 2, PADDED, LANES), f32),
            pltpu.VMEM((16, 2, ROWS, LANES), f32),
            pltpu.VMEM((16, 2, ROWS, LANES), f32),
            pltpu.VMEM((16, 2, PADDED, LANES), f32),
            pltpu.VMEM((16, 2, PADDED, LANES), f32),
            pltpu.VMEM((16, 2, PADDED, LANES), f32),
            pltpu.VMEM((10, COLOURS, 2, ROWS, LANES), f32),
            pltpu.VMEM((PHASES, 4, ROWS, LANES), f32),
            pltpu.VMEM((PHASES, 8, LANES), f32),
            pltpu.VMEM((4, TR, LANES), f32),
            pltpu.VMEM((16, LANES), f32),
            pltpu.VMEM((8, LANES), f32),
            dma((4, 4)),
            dma((16,)),
            dma((16,)),
            dma((4,)),
            dma((2,)),
            dma((2,)),
        ],
        compiler_params=pltpu.CompilerParams(collective_id=0, has_side_effects=True),
        name="gibbs",
    )(initial_field, information, kappa_squared, lumped_mass, noise_seeds.reshape(PHASES), colour_order)
    return final_field, energies[0, :PHASES].reshape(SWEEPS, COLOURS, 1)


def solution(mesh):
    placed = (
        P(None, "row", "col"),
        P("row", "col"),
        P("row", "col"),
        P("row", "col"),
        P("row", "col", None, None, None),
        P(),
    )
    return jax.shard_map(
        local, mesh=mesh, in_specs=placed, out_specs=(P(None, "row", "col"), P()), check_vma=False
    )
```

time: 590 us -> 47.1 us (0.08)
  local copies, waits for them, and re-layouts: 348 us -> 4.28 us
  other arithmetic: 96.1 us -> 0.66 us
  starting transfers between devices: 75.3 us -> 0 us
  Pallas kernels: 0 us -> 41 us
  blocking collectives: 32.3 us -> 0 us
  waiting for transfers between devices: 28.8 us -> 0 us
    slice x100 -> x1, local copies, waits for them, and re-layouts: 227 us -> 0.69 us  [local(): return (final_field, energies[0, :PHASES].reshape(SWEEPS, COLOURS, 1))]
    pad x32 -> x0, local copies, waits for them, and re-layouts: 103 us -> none  [join_corners(): padded = lax.pad(piece, jnp.zeros((), piece.dtype), config)]
    ppermute x40 -> x0, starting transfers between devices: 75.3 us -> none  [the longest x16 33.4 us: with_halo(): lax.ppermute(lax.slice_in_dim(block, 0, width, axis=dim), axis, backward)]
    pallas_call x0 -> x1, Pallas kernels: none -> 41 us  [local(): pl.pallas_call(kernel, out_shape=(jax.ShapeDtypeStruct((1, TR, TC), f32),...]
    select_n x20 -> x0, other arithmetic: 39.7 us -> none  [the longest x16 39.6 us: one_sweep(): jnp.where(chosen, updated[corner], before[corner])]
    psum x5 -> x0, blocking collectives: 32.3 us -> none  [one_axis_at_a_time(): shard = lax.psum(shard, axis)]
    ppermute x40 -> x0, waiting for transfers between devices: 28.8 us -> none  [the longest x16 16.5 us: with_halo(): lax.ppermute(lax.slice_in_dim(block, block.shape[dim] - width, None, axis...]
    another operation x10 -> x0, other arithmetic: 16.2 us -> none
  transfers between devices with their start and end apart: 40 -> 0, of which waited for: 17 -> 0; matrix products, arithmetic and copies ran while one was open for 19% -> 0% of each run, Pallas kernels for 0% -> 0%
where the time goes in v1:
time: 47.1 us; the launch traced here: 46.6 us
  Pallas kernels  41 us (87%)
  local copies, waits for them, and re-layouts  4.28 us (9%)
  other arithmetic  0.66 us (1%)
  between operations  0.65 us (1%)
    pallas_call x1, Pallas kernels, local(): pl.pallas_call(kernel, out_shape=(jax.ShapeDtypeStruct((1, TR, TC), f32),...  41 us
    unnamed x4, local copies, waits for them, and re-layouts  2.34 us

profile of v1, /device:TPU:1, one launch (start us, length us, event | category | flops | bytes accessed | tf_op | source)
XLA Modules:
  0.0 46.6 jit_solution(16143782522470555441)
XLA Ops:
  0.6 0.0 copy-start
  0.6 0.5 %broadcast.6 = s32[]{:T(128)} broadcast(s32[]{:T(128)} %constant.7), dimensions={} | broadcast | bytes 8 | tf_op args[4]
  1.2 0.2 copy-done
  1.3 0.7 %reduce.7 = s32[2,4]{1,0:T(2,128)S(1)} reduce(s32[1,1,2,4,1]{3,4,2,1,0:T(1,128)S(1)} %copy-done, s32[]{:T(128)} %broadcast.6), dimensions={0,1,4}, to_apply=%param.10.reduce_sub_computation.3 | reduce | bytes 68 | tf_op args[4]
  2.0 0.6 %reshape.7.seed_ref = s32[8]{0:T(128)} reshape(s32[2,4]{1,0:T(2,128)S(1)} %reduce.7) | data formatting | bytes 64 | tf_op jit(solution)/shard_map/reshape | solution.py:519
  2.6 41.0 %gibbs.1 = (f32[1,128,512]{2,1,0:T(8,128)}, f32[8,128]{1,0:T(8,128)}) custom-call(f32[1,128,512]{2,1,0:T(8,128)} %field_ref.1, f32[128,512]{1,0:T(8,128)} %info_ref.1, f32[128,512]{1,0:T(8,128)} %kappa_ref.1, f32[128,512]{1,0:T(8,128)} %mass_ref.1, s32[8]{0:T(128)} %reshape.7.seed_ref, s32[4]{0:T(128)} %order_ref.1), custom_call_target="tpu_custom_call" | custom-call | tf_op jit(solution)/shard_map/gibbs/pallas_call | solution.py:485
  43.6 0.7 %slice_reduce_fusion = f32[8]{0:T(128)S(1)} fusion(f32[8,128]{1,0:T(8,128)} %get-tuple-element.5), kind=kLoop, calls=%fused_computation | loop fusion | bytes 64 | tf_op jit(solution)/shard_map/slice | solution.py:520
  44.3 0.6 %reshape_squeeze.3 = f32[2,4,1]{1,0,2:T(2,128)} reshape(f32[8]{0:T(128)S(1)} %slice_reduce_fusion) | data formatting | bytes 64 | tf_op jit(solution)/shard_map/reshape;squeeze | solution.py:520
  44.9 1.7 %copy.10 = f32[1,128,512]{2,1,0:T(8,128)} copy(f32[1,128,512]{2,1,0:T(8,128)} %get-tuple-element.10) | data formatting | bytes 524288
Async XLA Ops:
  0.6 0.7 %copy-start = (s32[1,1,2,4,1]{3,4,2,1,0:T(1,128)S(1)}, s32[1,1,2,4,1]{3,4,2,1,0:T(1,128)}, u32[]{:S(2)}) copy-start(s32[1,1,2,4,1]{3,4,2,1,0:T(1,128)} %param.10) | copy-start | bytes 100

commit v2 on v1

--- a/solution.py
+++ b/solution.py
@@ -19,6 +19,7 @@
 PADDED = ROWS + 2 * PAD
 LANES = 128
 MIX = 73244475
+VMEM_LIMIT = 16 * 1024 * 1024
 STEP = 1.0 / 8388608.0
 NODES = 8388608.0
 NEIGHBOURS = [(a, b) for a in (-1, 0, 1) for b in (-1, 0, 1) if (a, b) != (0, 0)]
@@ -70,9 +71,9 @@
 
 
 def kernel(
-    field_ref, info_ref, kappa_ref, mass_ref, seed_ref, order_ref, out_ref, energy_ref,
-    nat, pack, strip_l, strip_r, seedbuf, seedmap, noise, fld, stf, inf, inv, scl, kd, fac, delta, acc, outn, e1, e2,
-    load_sem, send_sem, recv_sem, store_sem, esend, erecv,
+    field_ref, info_ref, kappa_ref, mass_ref, seed_ref, order_ref, outn, energy_ref,
+    nat, pack, strip_l, strip_r, seedbuf, seedmap, noise, fld, stf, inf, inv, scl, kd, fac, delta, acc, e1, e2,
+    load_sem, send_sem, recv_sem, esend, erecv,
 ):
     r, c = lax.axis_index("row"), lax.axis_index("col")
     sub, lane = tile()
@@ -81,8 +82,8 @@
         return (lax.rem(r + (dr + 8), 8), lax.rem(c + (dc + 16), 16))
 
     barrier = pltpu.get_barrier_semaphore()
-    peers = [at(0, k) for k in range(1, 16)] + [at(k, 0) for k in range(1, 8)]
-    peers += [at(a, b) for a in (-1, 1) for b in (-1, 1)]
+    peers = [at(*where) for where in NEIGHBOURS]
+    peers += [at(0, k) for k in range(2, 15)] + [at(k, 0) for k in range(2, 7)]
     for peer in peers:
         pl.semaphore_signal(barrier, inc=1, device_id=peer, device_id_type=MESH)
 
@@ -102,7 +103,7 @@
         for colour in range(COLOURS):
             seed = jnp.int32(0)
             for k in range(COLOURS):
-                seed = seed + jnp.where(order_ref[k] == colour, seed_ref[t * COLOURS + k], 0)
+                seed = seed + jnp.where(order_ref[k] == colour, seed_ref[t, 0, k], 0)
             own = jnp.where(sub == t * COLOURS + colour, seed, own)
     seedbuf[4] = own
 
@@ -162,6 +163,46 @@
 
     lax.fori_loop(0, 16, clear, 0)
 
+    block = lane // 32
+    split = [4 * (lane & 31) + ((block - k) & 3) for k in range(4)]
+    edge = lane < 64
+    used = (lane < 4) | (lane >= 124)
+
+    def keep(n, v, g, values):
+        rows = pl.ds(8 * g, 8)
+        padded = pl.ds(8 * g + PAD, 8)
+        fld[n, v, padded, :] = values[0]
+        inf[n, v, rows, :] = values[1]
+        stf[n, v, rows, :] = values[2] * values[3] + 4.0
+        inv[n, v, padded, :] = 1.0 / values[3]
+
+    def main_planes(g):
+        for rho in range(4):
+            natural = pl.ds(32 * g + rho, 8, stride=4)
+            values = []
+            for i in range(4):
+                chunks = [pick(split[k], nat[i, k, natural, :]) for k in range(4)]
+                row = []
+                for kappa in range(4):
+                    m = chunks[(-kappa) & 3]
+                    for b in range(1, 4):
+                        m = jnp.where(block == b, chunks[(b - kappa) & 3], m)
+                    row.append(pltpu.roll(m, LANES - 32 * kappa, 1) if kappa else m)
+                values.append(row)
+            for kappa in range(4):
+                keep(4 * rho + kappa, 0, g, [values[i][kappa] for i in range(4)])
+
+    def side_planes(g):
+        for rho in range(4):
+            natural = pl.ds(32 * g + rho, 8, stride=4)
+            mixed = jnp.where(edge, strip_l[natural, :], strip_r[natural, :])
+            for kappa in range(4):
+                values = []
+                for i in range(4):
+                    index = 16 * i + 4 * (lane & 3) + kappa + jnp.where(edge, 64, 0)
+                    values.append(jnp.where(used, pick(index, mixed), 0.0 if i < 2 else 1.0))
+                keep(4 * rho + kappa, 1, g, values)
+
     def draw(g, group_class, v):
         for rho in range(4):
             row = 4 * ((sub + (8 * g + 28)) & 31) + rho
@@ -202,44 +243,16 @@
 
     lax.fori_loop(0, GROUPS, side, 0)
 
-    for copy in copies[8:]:
+    for g in range(1, GROUPS - 1):
+        main_planes(g)
+    for copy in copies[8:14]:
         copy.wait()
-
-    block = lane // 32
-    split = [4 * (lane & 31) + ((block - k) & 3) for k in range(4)]
-    edge = lane < 64
-    used = (lane < 4) | (lane >= 124)
-
-    def planes(g, _):
-        rows = pl.ds(pl.multiple_of(8 * g, 8), 8)
-        padded = pl.ds(pl.multiple_of(8 * g + PAD, 8), 8)
-        for rho in range(4):
-            natural = pl.ds(32 * g + rho, 8, stride=4)
-            mixed = jnp.where(edge, strip_l[natural, :], strip_r[natural, :])
-            values = []
-            for i in range(4):
-                chunks = [pick(split[k], nat[i, k, natural, :]) for k in range(4)]
-                row = []
-                for kappa in range(4):
-                    m = chunks[(-kappa) & 3]
-                    for b in range(1, 4):
-                        m = jnp.where(block == b, chunks[(b - kappa) & 3], m)
-                    main = pltpu.roll(m, (LANES - 32 * kappa) % LANES, 1) if kappa else m
-                    index = jnp.where(edge, 64 + 16 * i + 4 * (lane & 3) + kappa, 16 * i + 4 * (lane & 3) + kappa)
-                    filler = 0.0 if i < 2 else 1.0
-                    row.append((main, jnp.where(used, pick(index, mixed), filler)))
-                values.append(row)
-            for kappa in range(4):
-                n = 4 * rho + kappa
-                for v in range(2):
-                    mass = values[3][kappa][v]
-                    fld[n, v, padded, :] = values[0][kappa][v]
-                    inf[n, v, rows, :] = values[1][kappa][v]
-                    stf[n, v, rows, :] = values[2][kappa][v] * mass + 4.0
-                    inv[n, v, padded, :] = 1.0 / mass
-        return 0
-
-    lax.fori_loop(0, GROUPS, planes, 0)
+    for g in range(GROUPS):
+        side_planes(g)
+    for copy in copies[14:]:
+        copy.wait()
+    for g in (0, GROUPS - 1):
+        main_planes(g)
 
     def around(ref, rho, kappa, base):
         up = (4 * ((rho + 3) % 4) + kappa, base - 1 if rho == 0 else base)
@@ -256,13 +269,19 @@
             for v in range(2)
         ]
 
+    def sweep(step):
+        total = zero
+        for g in range(GROUPS):
+            total = step(g, total)
+        return total
+
     def is_own(g):
         j = sub + 8 * g
         return (j >= 4) & (j < 36)
 
     def first(g, total):
-        base = pl.multiple_of(8 * g + PAD, 8)
-        rows = pl.ds(pl.multiple_of(8 * g, 8), 8)
+        base = 8 * g + PAD
+        rows = pl.ds(8 * g, 8)
         here = pl.ds(base, 8)
         part = zero
         for rho in range(4):
@@ -278,11 +297,11 @@
                         part = part + (0.5 * scaled * applied - inf[n, v, rows, :] * value)
         return total + jnp.where(is_own(g), part, 0.0)
 
-    acc[0] = lax.fori_loop(0, GROUPS, first, zero)
-
-    def factors(g, _):
-        base = pl.multiple_of(8 * g + PAD, 8)
-        rows = pl.ds(pl.multiple_of(8 * g, 8), 8)
+    acc[0] = sweep(first)
+
+    def factors(g):
+        base = 8 * g + PAD
+        rows = pl.ds(8 * g, 8)
         here = pl.ds(base, 8)
         for colour in range(COLOURS):
             top, left = 2 * (colour // 2), 2 * (colour % 2)
@@ -308,17 +327,17 @@
                     fac[n, colour, v, rows, :] = low[n, n]
                 for (a, b), n in LOWER.items():
                     fac[n, colour, v, rows, :] = low[a, b]
-        return 0
-
-    lax.fori_loop(0, GROUPS, factors, 0)
+
+    for g in range(GROUPS):
+        factors(g)
 
     def resample(i, g, total, scatter):
         t, k = i // COLOURS, lax.rem(i, COLOURS)
         colour = order_ref[k]
         a, b = lax.shift_right_logical(colour, 1), colour & 1
         low_b = jnp.full((8, LANES), b, jnp.int32) == 0
-        base = pl.multiple_of(8 * g + PAD, 8)
-        rows = pl.ds(pl.multiple_of(8 * g, 8), 8)
+        base = 8 * g + PAD
+        rows = pl.ds(8 * g, 8)
         here = pl.ds(base, 8)
         rel_row = [2 * a, 2 * a + 1, (2 * a + 2) & 3, (2 * a + 3) & 3]
         rel_col = [2 * b, 2 * b + 1, (2 * b + 2) & 3, (2 * b + 3) & 3]
@@ -392,7 +411,7 @@
     def spread(i, g):
         colour = order_ref[lax.rem(i, COLOURS)]
         a, b = lax.shift_right_logical(colour, 1), colour & 1
-        base = pl.multiple_of(8 * g + PAD, 8)
+        base = 8 * g + PAD
         here = pl.ds(base, 8)
         for rho in range(4):
             where = here
@@ -407,8 +426,9 @@
                     scl[n, v, here, :] = scl[n, v, here, :] - inv[n, v, here, :] * kd[place, v, where, :]
 
     def phase(i, _):
-        acc[i + 1] = lax.fori_loop(0, GROUPS, lambda g, total: resample(i, g, total, True), zero)
-        lax.fori_loop(0, GROUPS, lambda g, _: (spread(i, g), 0)[1], 0)
+        acc[i + 1] = sweep(lambda g, total: resample(i, g, total, True))
+        for g in range(GROUPS):
+            spread(i, g)
         return 0
 
     lax.fori_loop(0, PHASES - 1, phase, 0)
@@ -424,7 +444,7 @@
             device_id=at(0, k), device_id_type=MESH,
         ).start()
 
-    lax.fori_loop(0, GROUPS, lambda g, total: resample(PHASES - 1, g, total, False), zero)
+    sweep(lambda g, total: resample(PHASES - 1, g, total, False))
 
     turn_of = []
     for colour in range(COLOURS):
@@ -452,12 +472,6 @@
         return 0
 
     lax.fori_loop(0, 4, natural_rows, 0)
-    stores = [
-        pltpu.make_async_copy(outn.at[k], out_ref.at[0, :, pl.ds(LANES * k, LANES)], store_sem.at[k]) for k in range(4)
-    ]
-    for store in stores:
-        store.start()
-
     def finish(buffer, count, sem, where):
         pltpu.make_async_remote_copy(
             src_ref=buffer.at[pl.ds(0, count)], dst_ref=buffer.at[pl.ds(0, count)], send_sem=esend.at[sem],
@@ -473,20 +487,35 @@
         ).start()
     finish(e2, 7, 1, at(1, 0))
     energy_ref[...] = jnp.broadcast_to(jnp.sum(e2[...], axis=0, keepdims=True) * (1.0 / NODES), (8, LANES))
+
+
+def deliver(field_ref, energy_ref, out_ref, out_energy_ref, store_sem):
+    stores = [
+        pltpu.make_async_copy(field_ref.at[k], out_ref.at[0, :, pl.ds(LANES * k, LANES)], store_sem.at[k])
+        for k in range(4)
+    ]
+    for store in stores:
+        store.start()
+    line = energy_ref[0:1, :]
+    out_energy_ref[0] = line[:, 0:COLOURS]
+    out_energy_ref[1] = pltpu.roll(line, LANES - COLOURS, 1)[:, 0:COLOURS]
     for store in stores:
         store.wait()
 
 
 def local(initial_field, information, kappa_squared, lumped_mass, noise_seeds, colour_order):
     f32, i32 = jnp.float32, jnp.int32
-    anywhere = pl.BlockSpec(memory_space=pl.ANY)
+    anywhere = pl.BlockSpec(memory_space=pltpu.HBM)
     scalar = pl.BlockSpec(memory_space=pltpu.SMEM)
     dma = pltpu.SemaphoreType.DMA
-    final_field, energies = pl.pallas_call(
+    seeds = noise_seeds.reshape(SWEEPS, COLOURS, 1).transpose(0, 2, 1)
+    vmem = pl.BlockSpec(memory_space=pltpu.VMEM)
+    arrays = (initial_field, information, kappa_squared, lumped_mass)
+    chunks, line = pl.pallas_call(
         kernel,
-        out_shape=(jax.ShapeDtypeStruct((1, TR, TC), f32), jax.ShapeDtypeStruct((8, LANES), f32)),
+        out_shape=(jax.ShapeDtypeStruct((4, TR, LANES), f32), jax.ShapeDtypeStruct((8, LANES), f32)),
         in_specs=[anywhere] * 4 + [scalar] * 2,
-        out_specs=(anywhere, pl.BlockSpec(memory_space=pltpu.VMEM)),
+        out_specs=(vmem, vmem),
         scratch_shapes=[
             pltpu.VMEM((4, 4, EXT, LANES), f32),
             pltpu.VMEM((TR, LANES), f32),
@@ -504,20 +533,27 @@
             pltpu.VMEM((10, COLOURS, 2, ROWS, LANES), f32),
             pltpu.VMEM((PHASES, 4, ROWS, LANES), f32),
             pltpu.VMEM((PHASES, 8, LANES), f32),
-            pltpu.VMEM((4, TR, LANES), f32),
             pltpu.VMEM((16, LANES), f32),
             pltpu.VMEM((8, LANES), f32),
             dma((4, 4)),
             dma((16,)),
             dma((16,)),
-            dma((4,)),
             dma((2,)),
             dma((2,)),
         ],
-        compiler_params=pltpu.CompilerParams(collective_id=0, has_side_effects=True),
+        compiler_params=pltpu.CompilerParams(collective_id=0, has_side_effects=True, vmem_limit_bytes=VMEM_LIMIT),
         name="gibbs",
-    )(initial_field, information, kappa_squared, lumped_mass, noise_seeds.reshape(PHASES), colour_order)
-    return final_field, energies[0, :PHASES].reshape(SWEEPS, COLOURS, 1)
+    )(*(pltpu.with_memory_space_constraint(a, pltpu.HBM) for a in (*arrays, seeds, colour_order)))
+    final_field, energies = pl.pallas_call(
+        deliver,
+        out_shape=(jax.ShapeDtypeStruct((1, TR, TC), f32), jax.ShapeDtypeStruct((SWEEPS, 1, COLOURS), f32)),
+        in_specs=[vmem, vmem],
+        out_specs=(anywhere, vmem),
+        scratch_shapes=[dma((4,))],
+        compiler_params=pltpu.CompilerParams(vmem_limit_bytes=VMEM_LIMIT),
+        name="deliver",
+    )(chunks, line)
+    return final_field, energies.transpose(0, 2, 1)
 
 
 def solution(mesh):

time: 47.1 us -> 35.8 us (0.76)
  Pallas kernels: 41 us -> 34.8 us
  local copies, waits for them, and re-layouts: 4.28 us -> 0 us
  other arithmetic: 0.66 us -> 0 us
    pallas_call x1 -> x2, Pallas kernels: 41 us -> 34.8 us  [the longest x1 33.5 us: local(): pl.pallas_call(kernel, out_shape=(jax.ShapeDtypeStruct((4, TR, LANES), f3...]
    unnamed x4 -> x0, local copies, waits for them, and re-layouts: 2.34 us -> none
    slice x1 -> x0, local copies, waits for them, and re-layouts: 0.69 us -> none  [local(): return (final_field, energies[0, :PHASES].reshape(SWEEPS, COLOURS, 1))]
    unnamed x1 -> x0, other arithmetic: 0.66 us -> none
    another operation x1 -> x0, local copies, waits for them, and re-layouts: 0.64 us -> none  [local(): return (final_field, energies[0, :PHASES].reshape(SWEEPS, COLOURS, 1))]
    reshape x1 -> x0, local copies, waits for them, and re-layouts: 0.59 us -> none  [local(): noise_seeds.reshape(PHASES)]
where the time goes in v2:
time: 35.8 us; the launch traced here: 35.5 us
  Pallas kernels  34.8 us (97%)
  between operations  0.64 us (2%)
    pallas_call x1, Pallas kernels, local(): pl.pallas_call(kernel, out_shape=(jax.ShapeDtypeStruct((4, TR, LANES), f3...  33.5 us
    pallas_call x1, Pallas kernels, local(): pl.pallas_call(deliver, out_shape=(jax.ShapeDtypeStruct((1, TR, TC), f32)...  1.29 us

profile of v2, /device:TPU:1, one launch (start us, length us, event | category | flops | bytes accessed | tf_op | source)
XLA Modules:
  0.0 35.5 jit_solution(16260831848932236962)
XLA Ops:
  0.6 33.5 %gibbs.1 = (f32[4,128,128]{2,1,0:T(8,128)S(1)}, f32[8,128]{1,0:T(8,128)S(1)}) custom-call(f32[1,128,512]{2,1,0:T(8,128)} %field_ref.1, f32[128,512]{1,0:T(8,128)} %info_ref.1, f32[128,512]{1,0:T(8,128)} %kappa_ref.1, f32[128,512]{1,0:T(8,128)} %mass_ref.1, s32[2,1,4]{2,1,0:T(1,128)} %bitcast.6, s32[4]{0:T(128)} %order_ref.1), custom_call_target="tpu_custom_call" | custom-call | tf_op jit(solution)/shard_map/gibbs/pallas_call | solution.py:514
  34.2 1.3 %deliver.1 = (f32[1,128,512]{2,1,0:T(8,128)}, f32[2,1,4]{2,1,0:T(1,128)}) custom-call(f32[4,128,128]{2,1,0:T(8,128)S(1)} %get-tuple-element.6.field_ref, f32[8,128]{1,0:T(8,128)S(1)} %get-tuple-element.7.energy_ref), custom_call_target="tpu_custom_call" | custom-call | tf_op jit(solution)/shard_map/deliver/pallas_call | solution.py:547

commit v3 on v2

--- a/solution.py
+++ b/solution.py
@@ -19,9 +19,10 @@
 PADDED = ROWS + 2 * PAD
 LANES = 128
 MIX = 73244475
-VMEM_LIMIT = 16 * 1024 * 1024
+VMEM_LIMIT = 32 * 1024 * 1024
 STEP = 1.0 / 8388608.0
 NODES = 8388608.0
+DEVICES = 128
 NEIGHBOURS = [(a, b) for a in (-1, 0, 1) for b in (-1, 0, 1) if (a, b) != (0, 0)]
 LOWER = {(1, 0): 4, (2, 0): 5, (2, 1): 6, (3, 0): 7, (3, 1): 8, (3, 2): 9}
 SINE = (6.283185307179586, -41.34170224039976, 81.60524927607506, -76.70585975306136, 42.05869394489765, -15.09464257682298, 3.8199525848482803)
@@ -72,8 +73,8 @@
 
 def kernel(
     field_ref, info_ref, kappa_ref, mass_ref, seed_ref, order_ref, outn, energy_ref,
-    nat, pack, strip_l, strip_r, seedbuf, seedmap, noise, fld, stf, inf, inv, scl, kd, fac, delta, acc, e1, e2,
-    load_sem, send_sem, recv_sem, esend, erecv,
+    nat, halo, turned_nat, edge_planes, pack, strip_l, strip_r, seedbuf, seedmap, noise, fld, stf, inf, inv, scl, kd, fac, delta, acc, sums,
+    load_sem, send_sem, recv_sem, esend, erecv, known,
 ):
     r, c = lax.axis_index("row"), lax.axis_index("col")
     sub, lane = tile()
@@ -147,20 +148,38 @@
         theirs = {-1: pl.ds(HALO + TR, HALO), 0: pl.ds(HALO, TR), 1: pl.ds(0, HALO)}[dr]
         send(pack.at[mine], strip_l.at[theirs], (dr, 1))
         send(pack.at[mine], strip_r.at[theirs], (dr, -1))
-    send(nat.at[:, :, pl.ds(HALO, HALO)], nat.at[:, :, pl.ds(HALO + TR, HALO)], (-1, 0))
-    send(nat.at[:, :, pl.ds(TR, HALO)], nat.at[:, :, pl.ds(0, HALO)], (1, 0))
+    send(nat.at[:, :, pl.ds(HALO, HALO)], halo.at[1, :, :, pl.ds(HALO, HALO)], (-1, 0))
+    send(nat.at[:, :, pl.ds(TR, HALO)], halo.at[0, :, :, pl.ds(0, HALO)], (1, 0))
+    for k in range(1, 8):
+        pl.semaphore_signal(known, inc=1, device_id=at(k, 0), device_id_type=MESH)
 
     zero = jnp.zeros((8, LANES), jnp.float32)
 
+    one = jnp.ones((8, LANES), jnp.float32)
+
     def clear(n, _):
+        for i in range(4):
+            nat[i, lax.rem(n, 4), pl.ds(pl.multiple_of(8 * (n // 4) + jnp.where(n >= 8, TR, 0), 8), 8), :] = one
         for v in range(2):
-            for buffer in (fld, inv, scl, kd):
+            for buffer in (fld, inv):
                 buffer[n, v, 0:PAD, :] = zero
                 buffer[n, v, PAD + ROWS : PADDED, :] = zero
-            for g in range(GROUPS):
-                kd[n, v, PAD + 8 * g : PAD + 8 * g + 8, :] = zero
-        return 0
-
+            for i in range(PHASES):
+                scl[i, n, v, 0:PAD, :] = zero
+                scl[i, n, v, PAD + ROWS : PADDED, :] = zero
+        return 0
+
+    def clear_moves(i, _):
+        for n in range(16):
+            for v in range(2):
+                kd[i, n, v, 0:PAD, :] = zero
+                kd[i, n, v, PAD + ROWS : PADDED, :] = zero
+                if n in (10, 11, 14, 15):
+                    for g in range(GROUPS):
+                        kd[i, n, v, PAD + 8 * g : PAD + 8 * g + 8, :] = zero
+        return 0
+
+    lax.fori_loop(0, PHASES - 1, clear_moves, 0)
     lax.fori_loop(0, 16, clear, 0)
 
     block = lane // 32
@@ -168,40 +187,54 @@
     edge = lane < 64
     used = (lane < 4) | (lane >= 124)
 
-    def keep(n, v, g, values):
+    def finish_planes(g, v):
         rows = pl.ds(8 * g, 8)
         padded = pl.ds(8 * g + PAD, 8)
-        fld[n, v, padded, :] = values[0]
-        inf[n, v, rows, :] = values[1]
-        stf[n, v, rows, :] = values[2] * values[3] + 4.0
-        inv[n, v, padded, :] = 1.0 / values[3]
-
-    def main_planes(g):
+        for n in range(16):
+            mass = inv[n, v, padded, :]
+            stf[n, v, rows, :] = stf[n, v, rows, :] * mass + 4.0
+            inv[n, v, padded, :] = 1.0 / mass
+
+    def place_of(g):
+        rows, padded = pl.ds(8 * g, 8), pl.ds(8 * g + PAD, 8)
+        return (fld, padded), (inf, rows), (stf, rows), (inv, padded)
+
+    def gather_columns(g, load):
         for rho in range(4):
-            natural = pl.ds(32 * g + rho, 8, stride=4)
-            values = []
             for i in range(4):
-                chunks = [pick(split[k], nat[i, k, natural, :]) for k in range(4)]
-                row = []
+                for k in range(4):
+                    turned_nat[g, i, rho, k] = pick(split[k], load(i, k, rho))
+
+    def turn_columns(g, part=None):
+        for rho in range(4):
+            for i, (ref, where) in enumerate(place_of(g)):
+                chunks = [turned_nat[g, i, rho, k] for k in range(4)]
                 for kappa in range(4):
                     m = chunks[(-kappa) & 3]
                     for b in range(1, 4):
                         m = jnp.where(block == b, chunks[(b - kappa) & 3], m)
-                    row.append(pltpu.roll(m, LANES - 32 * kappa, 1) if kappa else m)
-                values.append(row)
-            for kappa in range(4):
-                keep(4 * rho + kappa, 0, g, [values[i][kappa] for i in range(4)])
+                    m = pltpu.roll(m, LANES - 32 * kappa, 1) if kappa else m
+                    if part is None:
+                        ref[4 * rho + kappa, 0, where, :] = m
+                    else:
+                        edge_planes[i, 4 * rho + kappa, g // 4] = m
+
+    def blend(g, part):
+        rows, padded = pl.ds(8 * g, 8), pl.ds(8 * g + PAD, 8)
+        for n in range(16):
+            mass = edge_planes[3, n, g // 4]
+            new = (edge_planes[0, n, g // 4], edge_planes[1, n, g // 4], edge_planes[2, n, g // 4] * mass + 4.0, 1.0 / mass)
+            for ref, where, value in zip((fld, inf, stf, inv), (padded, rows, rows, padded), new):
+                ref[n, 0, where, :] = jnp.where(part, value, ref[n, 0, where, :])
 
     def side_planes(g):
         for rho in range(4):
             natural = pl.ds(32 * g + rho, 8, stride=4)
             mixed = jnp.where(edge, strip_l[natural, :], strip_r[natural, :])
             for kappa in range(4):
-                values = []
-                for i in range(4):
+                for i, (ref, where) in enumerate(place_of(g)):
                     index = 16 * i + 4 * (lane & 3) + kappa + jnp.where(edge, 64, 0)
-                    values.append(jnp.where(used, pick(index, mixed), 0.0 if i < 2 else 1.0))
-                keep(4 * rho + kappa, 1, g, values)
+                    ref[4 * rho + kappa, 1, where, :] = jnp.where(used, pick(index, mixed), 0.0 if i < 2 else 1.0)
 
     def draw(g, group_class, v):
         for rho in range(4):
@@ -243,16 +276,18 @@
 
     lax.fori_loop(0, GROUPS, side, 0)
 
-    for g in range(1, GROUPS - 1):
-        main_planes(g)
+    for g in range(GROUPS):
+        gather_columns(g, lambda i, k, rho, g=g: nat[i, k, pl.ds(32 * g + rho, 8, stride=4), :])
+    for g in range(GROUPS):
+        turn_columns(g)
+    for g in range(GROUPS):
+        finish_planes(g, 0)
     for copy in copies[8:14]:
         copy.wait()
     for g in range(GROUPS):
         side_planes(g)
-    for copy in copies[14:]:
-        copy.wait()
-    for g in (0, GROUPS - 1):
-        main_planes(g)
+    for g in range(GROUPS):
+        finish_planes(g, 1)
 
     def around(ref, rho, kappa, base):
         up = (4 * ((rho + 3) % 4) + kappa, base - 1 if rho == 0 else base)
@@ -269,12 +304,6 @@
             for v in range(2)
         ]
 
-    def sweep(step):
-        total = zero
-        for g in range(GROUPS):
-            total = step(g, total)
-        return total
-
     def is_own(g):
         j = sub + 8 * g
         return (j >= 4) & (j < 36)
@@ -292,12 +321,11 @@
                     value = fld[n, v, here, :]
                     applied = stf[n, v, rows, :] * value - near[v]
                     scaled = inv[n, v, here, :] * applied
-                    scl[n, v, here, :] = scaled
+                    scl[0, n, v, here, :] = scaled
                     if v == 0:
                         part = part + (0.5 * scaled * applied - inf[n, v, rows, :] * value)
         return total + jnp.where(is_own(g), part, 0.0)
 
-    acc[0] = sweep(first)
 
     def factors(g):
         base = 8 * g + PAD
@@ -328,8 +356,6 @@
                 for (a, b), n in LOWER.items():
                     fac[n, colour, v, rows, :] = low[a, b]
 
-    for g in range(GROUPS):
-        factors(g)
 
     def resample(i, g, total, scatter):
         t, k = i // COLOURS, lax.rem(i, COLOURS)
@@ -345,7 +371,7 @@
         below = pl.ds(base + jnp.where(a == 1, 1, 0), 8)
 
         def read(p, q, where=here):
-            return [scl[4 * rel_row[p] + rel_col[q], v, where, :] for v in range(2)]
+            return [scl[i, 4 * rel_row[p] + rel_col[q], v, where, :] for v in range(2)]
 
         node = [[read(p, q) for q in range(2)] for p in range(2)]
         up = [read(3, q, above) for q in range(2)]
@@ -391,21 +417,21 @@
                 for n in range(4):
                     p, q = n // 2, n % 2
                     place = 4 * rel_row[p] + rel_col[q]
-                    kd[4 * p + q, v, here, :] = move[n ^ 1] + move[n ^ 2] - stf[place, v, rows, :] * move[n]
+                    kd[i, 4 * p + q, v, here, :] = move[n ^ 1] + move[n ^ 2] - stf[place, v, rows, :] * move[n]
                 for q in range(2):
-                    kd[12 + q, v, here, :] = move[q]
-                    kd[8 + q, v, here, :] = move[2 + q]
+                    kd[i, 12 + q, v, here, :] = move[q]
+                    kd[i, 8 + q, v, here, :] = move[2 + q]
             moves.append(move)
         if scatter:
             for p in range(2):
                 raw = [moves[v][2 * p] for v in range(2)]
                 moved = lane_next(*raw, lane)
                 for v in range(2):
-                    kd[4 * p + 3, v, here, :] = jnp.where(low_b, moved[v], raw[v])
+                    kd[i, 4 * p + 3, v, here, :] = jnp.where(low_b, moved[v], raw[v])
                 raw = [moves[v][2 * p + 1] for v in range(2)]
                 moved = lane_prev(*raw, lane)
                 for v in range(2):
-                    kd[4 * p + 2, v, here, :] = jnp.where(low_b, raw[v], moved[v])
+                    kd[i, 4 * p + 2, v, here, :] = jnp.where(low_b, raw[v], moved[v])
         return total
 
     def spread(i, g):
@@ -423,28 +449,66 @@
                 n = 4 * rho + kappa
                 place = 4 * ((rho + 4 - 2 * a) & 3) + ((kappa + 4 - 2 * b) & 3)
                 for v in range(2):
-                    scl[n, v, here, :] = scl[n, v, here, :] - inv[n, v, here, :] * kd[place, v, where, :]
-
-    def phase(i, _):
-        acc[i + 1] = sweep(lambda g, total: resample(i, g, total, True))
-        for g in range(GROUPS):
+                    scl[i + 1, n, v, here, :] = scl[i, n, v, here, :] - inv[n, v, here, :] * kd[i, place, v, where, :]
+
+    inside, rim, every = range(1, GROUPS - 1), (0, GROUPS - 1), range(GROUPS)
+
+    def phase(i, groups, counted):
+        total = zero
+        for g in groups:
+            change = resample(i, g, zero, True)
+            total = total + change if g in counted else total
+        acc[i + 1] = total if counted is inside else acc[i + 1] + total
+        for g in groups:
             spread(i, g)
         return 0
 
-    lax.fori_loop(0, PHASES - 1, phase, 0)
+    total = zero
+    for g in every:
+        part = first(g, zero)
+        total = total + part if g in inside else total
+    acc[0] = total
+    for g in every:
+        factors(g)
+    lax.fori_loop(0, PHASES - 1, lambda i, _: phase(i, every, inside), 0)
+    for g in inside:
+        resample(PHASES - 1, g, zero, False)
+
+    for copy in copies[14:]:
+        copy.wait()
+    for g, side in ((0, 0), (GROUPS - 1, 1)):
+        gather_columns(g, lambda i, k, rho, side=side: halo[side, i, k, pl.ds(rho, 8, stride=4), :])
+    for g in rim:
+        turn_columns(g, True)
+    blend(0, sub < 4)
+    blend(GROUPS - 1, sub >= 4)
+    for g in rim:
+        acc[0] = first(g, acc[0])
+    for g in rim:
+        factors(g)
+    lax.fori_loop(0, PHASES - 1, lambda i, _: phase(i, rim, rim), 0)
 
     line = jnp.zeros((1, LANES), jnp.float32)
     for k in range(PHASES):
         change = jnp.sum(jnp.sum(acc[k], axis=0, keepdims=True), axis=1, keepdims=True)
         line = line + jnp.where(lane[0:1] >= k, change, 0.0)
-    e1[pl.ds(c, 1), :] = line
-    for k in range(1, 16):
+    me = 16 * r + c
+    mine = sums.at[pl.ds(me, 1)]
+    sums[pl.ds(me, 1), :] = line
+    pl.semaphore_wait(known, 7)
+
+    def share(k, _):
+        other = lax.rem(me + k, DEVICES)
         pltpu.make_async_remote_copy(
-            src_ref=e1.at[pl.ds(c, 1)], dst_ref=e1.at[pl.ds(c, 1)], send_sem=esend.at[0], recv_sem=erecv.at[0],
-            device_id=at(0, k), device_id_type=MESH,
+            src_ref=mine, dst_ref=mine, send_sem=esend, recv_sem=erecv,
+            device_id=(other // 16, lax.rem(other, 16)), device_id_type=MESH,
         ).start()
-
-    sweep(lambda g, total: resample(PHASES - 1, g, total, False))
+        return 0
+
+    lax.fori_loop(1, DEVICES, share, 0)
+
+    for g in rim:
+        resample(PHASES - 1, g, zero, False)
 
     turn_of = []
     for colour in range(COLOURS):
@@ -472,21 +536,11 @@
         return 0
 
     lax.fori_loop(0, 4, natural_rows, 0)
-    def finish(buffer, count, sem, where):
-        pltpu.make_async_remote_copy(
-            src_ref=buffer.at[pl.ds(0, count)], dst_ref=buffer.at[pl.ds(0, count)], send_sem=esend.at[sem],
-            recv_sem=erecv.at[sem], device_id=where, device_id_type=MESH,
-        ).wait()
-
-    finish(e1, 15, 0, at(0, 1))
-    e2[pl.ds(r, 1), :] = jnp.sum(e1[...], axis=0, keepdims=True)
-    for k in range(1, 8):
-        pltpu.make_async_remote_copy(
-            src_ref=e2.at[pl.ds(r, 1)], dst_ref=e2.at[pl.ds(r, 1)], send_sem=esend.at[1], recv_sem=erecv.at[1],
-            device_id=at(k, 0), device_id_type=MESH,
-        ).start()
-    finish(e2, 7, 1, at(1, 0))
-    energy_ref[...] = jnp.broadcast_to(jnp.sum(e2[...], axis=0, keepdims=True) * (1.0 / NODES), (8, LANES))
+    others = sums.at[pl.ds(0, DEVICES - 1)]
+    pltpu.make_async_remote_copy(
+        src_ref=others, dst_ref=others, send_sem=esend, recv_sem=erecv, device_id=at(0, 1), device_id_type=MESH
+    ).wait()
+    energy_ref[...] = jnp.broadcast_to(jnp.sum(sums[...], axis=0, keepdims=True) * (1.0 / NODES), (8, LANES))
 
 
 def deliver(field_ref, energy_ref, out_ref, out_energy_ref, store_sem):
@@ -518,6 +572,9 @@
         out_specs=(vmem, vmem),
         scratch_shapes=[
             pltpu.VMEM((4, 4, EXT, LANES), f32),
+            pltpu.VMEM((2, 4, 4, 2 * HALO, LANES), f32),
+            pltpu.VMEM((GROUPS, 4, 4, 4, 8, LANES), f32),
+            pltpu.VMEM((4, 16, 2, 8, LANES), f32),
             pltpu.VMEM((TR, LANES), f32),
             pltpu.VMEM((EXT, LANES), f32),
             pltpu.VMEM((EXT, LANES), f32),
@@ -528,18 +585,18 @@
             pltpu.VMEM((16, 2, ROWS, LANES), f32),
             pltpu.VMEM((16, 2, ROWS, LANES), f32),
             pltpu.VMEM((16, 2, PADDED, LANES), f32),
-            pltpu.VMEM((16, 2, PADDED, LANES), f32),
-            pltpu.VMEM((16, 2, PADDED, LANES), f32),
+            pltpu.VMEM((PHASES, 16, 2, PADDED, LANES), f32),
+            pltpu.VMEM((PHASES - 1, 16, 2, PADDED, LANES), f32),
             pltpu.VMEM((10, COLOURS, 2, ROWS, LANES), f32),
             pltpu.VMEM((PHASES, 4, ROWS, LANES), f32),
             pltpu.VMEM((PHASES, 8, LANES), f32),
-            pltpu.VMEM((16, LANES), f32),
-            pltpu.VMEM((8, LANES), f32),
+            pltpu.VMEM((DEVICES, LANES), f32),
             dma((4, 4)),
             dma((16,)),
             dma((16,)),
-            dma((2,)),
-            dma((2,)),
+            dma,
+            dma,
+            pltpu.SemaphoreType.REGULAR,
         ],
         compiler_params=pltpu.CompilerParams(collective_id=0, has_side_effects=True, vmem_limit_bytes=VMEM_LIMIT),
         name="gibbs",

time: 35.8 us -> 32.8 us (0.916)
  Pallas kernels: 34.8 us -> 32 us
    pallas_call x1, Pallas kernels: 33.5 us -> 30.7 us  [local(): pl.pallas_call(kernel, out_shape=(jax.ShapeDtypeStruct((4, TR, LANES), f3...]
where the time goes in v3:
time: 32.8 us; the launch traced here: 32.6 us
  Pallas kernels  32 us (98%)
  between operations  0.64 us (2%)
    pallas_call x1, Pallas kernels, local(): pl.pallas_call(kernel, out_shape=(jax.ShapeDtypeStruct((4, TR, LANES), f3...  30.7 us
    pallas_call x1, Pallas kernels, local(): pl.pallas_call(deliver, out_shape=(jax.ShapeDtypeStruct((1, TR, TC), f32)...  1.29 us

profile of v3, /device:TPU:1, one launch (start us, length us, event | category | flops | bytes accessed | tf_op | source)
XLA Modules:
  0.0 32.6 jit_solution(834783758055469741)
XLA Ops:
  0.6 30.7 %gibbs.1 = (f32[4,128,128]{2,1,0:T(8,128)S(1)}, f32[8,128]{1,0:T(8,128)S(1)}) custom-call(f32[1,128,512]{2,1,0:T(8,128)} %field_ref.1, f32[128,512]{1,0:T(8,128)} %info_ref.1, f32[128,512]{1,0:T(8,128)} %kappa_ref.1, f32[128,512]{1,0:T(8,128)} %mass_ref.1, s32[2,1,4]{2,1,0:T(1,128)} %bitcast.6, s32[4]{0:T(128)} %order_ref.1), custom_call_target="tpu_custom_call" | custom-call | tf_op jit(solution)/shard_map/gibbs/pallas_call | solution.py:568
  31.3 1.3 %deliver.1 = (f32[1,128,512]{2,1,0:T(8,128)}, f32[2,1,4]{2,1,0:T(1,128)}) custom-call(f32[4,128,128]{2,1,0:T(8,128)S(1)} %get-tuple-element.6.field_ref, f32[8,128]{1,0:T(8,128)S(1)} %get-tuple-element.7.energy_ref), custom_call_target="tpu_custom_call" | custom-call | tf_op jit(solution)/shard_map/deliver/pallas_call | solution.py:604

commit v4 on v3

--- a/solution.py
+++ b/solution.py
@@ -85,7 +85,7 @@
     barrier = pltpu.get_barrier_semaphore()
     peers = [at(*where) for where in NEIGHBOURS]
     peers += [at(0, k) for k in range(2, 15)] + [at(k, 0) for k in range(2, 7)]
-    for peer in peers:
+    for peer in peers[:8]:
         pl.semaphore_signal(barrier, inc=1, device_id=peer, device_id_type=MESH)
 
     sources = (field_ref.at[0], info_ref, kappa_ref, mass_ref)
@@ -99,6 +99,9 @@
             )
             loads[-1].start()
 
+    for peer in peers[8:]:
+        pl.semaphore_signal(barrier, inc=1, device_id=peer, device_id_type=MESH)
+
     own = jnp.zeros((8, LANES), jnp.int32)
     for t in range(SWEEPS):
         for colour in range(COLOURS):
@@ -107,22 +110,6 @@
                 seed = seed + jnp.where(order_ref[k] == colour, seed_ref[t, 0, k], 0)
             own = jnp.where(sub == t * COLOURS + colour, seed, own)
     seedbuf[4] = own
-
-    for load in loads:
-        load.wait()
-
-    def pack_rows(g, _):
-        rows = pl.ds(HALO + 8 * g, 8)
-        total = jnp.zeros((8, LANES), jnp.float32)
-        for i in range(4):
-            right = pltpu.roll(nat[i, 3, rows, :], 16 * i + 16, 1)
-            left = pltpu.roll(nat[i, 0, rows, :], 64 + 16 * i, 1)
-            total = jnp.where((lane >= 16 * i) & (lane < 16 * i + 16), right, total)
-            total = jnp.where((lane >= 64 + 16 * i) & (lane < 80 + 16 * i), left, total)
-        pack[pl.ds(8 * g, 8), :] = total
-        return 0
-
-    lax.fori_loop(0, TR // 8, pack_rows, 0)
 
     pl.semaphore_wait(barrier, len(peers))
     copies = []
@@ -143,6 +130,22 @@
 
     for dr, dc in NEIGHBOURS:
         send(seedbuf.at[4], seedbuf.at[(1 - dr) * 3 + 1 - dc], (dr, dc))
+    for load in loads:
+        load.wait()
+    for g in range(TR // 8):
+        rows = pl.ds(HALO + 8 * g, 8)
+        total = jnp.zeros((8, LANES), jnp.float32)
+        for i in range(4):
+            right = pltpu.roll(nat[i, 3, rows, :], 16 * i + 16, 1)
+            left = pltpu.roll(nat[i, 0, rows, :], 64 + 16 * i, 1)
+            total = jnp.where((lane >= 16 * i) & (lane < 16 * i + 16), right, total)
+            total = jnp.where((lane >= 64 + 16 * i) & (lane < 80 + 16 * i), left, total)
+        pack[pl.ds(8 * g, 8), :] = total
+    def splat(slot, n):
+        return jnp.broadcast_to(seedbuf[slot, n : n + 1, :], (8, LANES))
+
+    for n in range(8):
+        seedmap[n, 0, 1] = splat(4, n)
     for dr in (-1, 0, 1):
         mine = {-1: pl.ds(0, HALO), 0: pl.ds(0, TR), 1: pl.ds(TR - HALO, HALO)}[dr]
         theirs = {-1: pl.ds(HALO + TR, HALO), 0: pl.ds(HALO, TR), 1: pl.ds(0, HALO)}[dr]
@@ -246,18 +249,18 @@
                     seeds = seedmap[t * COLOURS + colour, v, group_class]
                     noise[t, 4 * rho + kappa, v, pl.ds(pl.multiple_of(8 * g, 8), 8), :] = gaussian(seeds + offset)
 
-    def splat(slot, n):
-        return jnp.broadcast_to(seedbuf[slot, n : n + 1, :], (8, LANES))
-
-    for n in range(8):
-        seedmap[n, 0, 1] = splat(4, n)
-
     def inner(g, _):
         draw(g, 1, 0)
         return 0
 
     lax.fori_loop(1, GROUPS - 1, inner, 0)
 
+    for g in range(GROUPS):
+        gather_columns(g, lambda i, k, rho, g=g: nat[i, k, pl.ds(32 * g + rho, 8, stride=4), :])
+    for g in range(GROUPS):
+        turn_columns(g)
+    for g in range(GROUPS):
+        finish_planes(g, 0)
     for copy in copies[:8]:
         copy.wait()
     for n in range(8):
@@ -276,12 +279,6 @@
 
     lax.fori_loop(0, GROUPS, side, 0)
 
-    for g in range(GROUPS):
-        gather_columns(g, lambda i, k, rho, g=g: nat[i, k, pl.ds(32 * g + rho, 8, stride=4), :])
-    for g in range(GROUPS):
-        turn_columns(g)
-    for g in range(GROUPS):
-        finish_planes(g, 0)
     for copy in copies[8:14]:
         copy.wait()
     for g in range(GROUPS):

time: 32.8 us -> 31.5 us (0.960)
  Pallas kernels: 32 us -> 30.8 us
    pallas_call x1, Pallas kernels: 30.7 us -> 29.5 us  [local(): pl.pallas_call(kernel, out_shape=(jax.ShapeDtypeStruct((4, TR, LANES), f3...]
where the time goes in v4:
time: 31.5 us; the launch traced here: 31.4 us
  Pallas kernels  30.8 us (98%)
  between operations  0.64 us (2%)
    pallas_call x1, Pallas kernels, local(): pl.pallas_call(kernel, out_shape=(jax.ShapeDtypeStruct((4, TR, LANES), f3...  29.5 us
    pallas_call x1, Pallas kernels, local(): pl.pallas_call(deliver, out_shape=(jax.ShapeDtypeStruct((1, TR, TC), f32)...  1.29 us

profile of v4, /device:TPU:1, one launch (start us, length us, event | category | flops | bytes accessed | tf_op | source)
XLA Modules:
  0.0 31.4 jit_solution(5793265211389240404)
XLA Ops:
  0.6 29.5 %gibbs.1 = (f32[4,128,128]{2,1,0:T(8,128)S(1)}, f32[8,128]{1,0:T(8,128)S(1)}) custom-call(f32[1,128,512]{2,1,0:T(8,128)} %field_ref.1, f32[128,512]{1,0:T(8,128)} %info_ref.1, f32[128,512]{1,0:T(8,128)} %kappa_ref.1, f32[128,512]{1,0:T(8,128)} %mass_ref.1, s32[2,1,4]{2,1,0:T(1,128)} %bitcast.6, s32[4]{0:T(128)} %order_ref.1), custom_call_target="tpu_custom_call" | custom-call | tf_op jit(solution)/shard_map/gibbs/pallas_call | solution.py:565
  30.1 1.3 %deliver.1 = (f32[1,128,512]{2,1,0:T(8,128)}, f32[2,1,4]{2,1,0:T(1,128)}) custom-call(f32[4,128,128]{2,1,0:T(8,128)S(1)} %get-tuple-element.6.field_ref, f32[8,128]{1,0:T(8,128)S(1)} %get-tuple-element.7.energy_ref), custom_call_target="tpu_custom_call" | custom-call | tf_op jit(solution)/shard_map/deliver/pallas_call | solution.py:601

commit v5 on v4

--- a/solution.py
+++ b/solution.py
@@ -468,8 +468,6 @@
     for g in every:
         factors(g)
     lax.fori_loop(0, PHASES - 1, lambda i, _: phase(i, every, inside), 0)
-    for g in inside:
-        resample(PHASES - 1, g, zero, False)
 
     for copy in copies[14:]:
         copy.wait()
@@ -495,16 +493,19 @@
     pl.semaphore_wait(known, 7)
 
     def share(k, _):
-        other = lax.rem(me + k, DEVICES)
-        pltpu.make_async_remote_copy(
-            src_ref=mine, dst_ref=mine, send_sem=esend, recv_sem=erecv,
-            device_id=(other // 16, lax.rem(other, 16)), device_id_type=MESH,
-        ).start()
+        row, col = lax.rem(k, 32) // 4, 8 * lax.rem(k // 2, 2) + 2 * (k // 32) + lax.rem(k, 2)
+
+        @pl.when(16 * row + col != me)
+        def _():
+            pltpu.make_async_remote_copy(
+                src_ref=mine, dst_ref=mine, send_sem=esend, recv_sem=erecv, device_id=(row, col), device_id_type=MESH
+            ).start()
+
         return 0
 
-    lax.fori_loop(1, DEVICES, share, 0)
-
-    for g in rim:
+    lax.fori_loop(0, DEVICES, share, 0)
+
+    for g in every:
         resample(PHASES - 1, g, zero, False)
 
     turn_of = []

time: 31.5 us -> 31.1 us (0.987)
  Pallas kernels: 30.8 us -> 30.3 us
    pallas_call x1, Pallas kernels: 29.5 us -> 29 us  [local(): pl.pallas_call(kernel, out_shape=(jax.ShapeDtypeStruct((4, TR, LANES), f3...]
where the time goes in v5:
time: 31.1 us; the launch traced here: 31 us
  Pallas kernels  30.3 us (97%)
  between operations  0.64 us (2%)
    pallas_call x1, Pallas kernels, local(): pl.pallas_call(kernel, out_shape=(jax.ShapeDtypeStruct((4, TR, LANES), f3...  29 us
    pallas_call x1, Pallas kernels, local(): pl.pallas_call(deliver, out_shape=(jax.ShapeDtypeStruct((1, TR, TC), f32)...  1.29 us

profile of v5, /device:TPU:1, one launch (start us, length us, event | category | flops | bytes accessed | tf_op | source)
XLA Modules:
  0.0 31.0 jit_solution(234064274077724764)
XLA Ops:
  0.6 29.0 %gibbs.1 = (f32[4,128,128]{2,1,0:T(8,128)S(1)}, f32[8,128]{1,0:T(8,128)S(1)}) custom-call(f32[1,128,512]{2,1,0:T(8,128)} %field_ref.1, f32[128,512]{1,0:T(8,128)} %info_ref.1, f32[128,512]{1,0:T(8,128)} %kappa_ref.1, f32[128,512]{1,0:T(8,128)} %mass_ref.1, s32[2,1,4]{2,1,0:T(1,128)} %bitcast.6, s32[4]{0:T(128)} %order_ref.1), custom_call_target="tpu_custom_call" | custom-call | tf_op jit(solution)/shard_map/gibbs/pallas_call | solution.py:566
  29.7 1.3 %deliver.1 = (f32[1,128,512]{2,1,0:T(8,128)}, f32[2,1,4]{2,1,0:T(1,128)}) custom-call(f32[4,128,128]{2,1,0:T(8,128)S(1)} %get-tuple-element.6.field_ref, f32[8,128]{1,0:T(8,128)S(1)} %get-tuple-element.7.energy_ref), custom_call_target="tpu_custom_call" | custom-call | tf_op jit(solution)/shard_map/deliver/pallas_call | solution.py:602
